TPU v7x, 32 devices: a whole 2x2x4 slice. The times are simulated.
32 devices in a mesh: dp: 8 (over z, y), tensor: 4 (over x, core).
Axes of the slice: x: 2, y: 2, z: 4, core: 2. Of those that a mesh axis runs over, the one named last changes fastest.
Arguments:
- image_rows: bfloat16 [16, 197, 768], P('dp', None, 'tensor'), may hold values from -6 to 6
- text_rows: bfloat16 [8, 512, 768], P('dp', None, 'tensor'), may hold values from -6 to 6
- pair_rows: bfloat16 [8, 711, 768], P('dp', None, 'tensor'), may hold values from -6 to 6
- text_lengths: int32 [8], P('dp'), may hold values from 128 to 512, as said below
- pair_lengths: int32 [8], P('dp'), may hold values from 128 to 512, as said below
- qkv_weight: bfloat16 [3, 768, 3, 768], P(None, None, None, 'tensor'), may hold values from -0.21875 to 0.21875
- qv_bias: bfloat16 [3, 2, 768], P(None, None, 'tensor'), may hold values from -3 to 3
- out_weight: bfloat16 [3, 768, 768], P(None, 'tensor'), may hold values from -3.5 to 3.5
- out_bias: bfloat16 [3, 768], P(None, 'tensor'), may hold values from -3 to 3
- up_weight: bfloat16 [3, 768, 3072], P(None, None, 'tensor'), may hold values from -0.21875 to 0.21875
- up_bias: bfloat16 [3, 3072], P(None, 'tensor'), may hold values from -3 to 3
- down_weight: bfloat16 [3, 3072, 768], P(None, 'tensor'), may hold values from -0.109375 to 0.109375
- down_bias: bfloat16 [3, 768], P(None, 'tensor'), may hold values from -3 to 3
- norm_gain: bfloat16 [3, 2, 768], P(None, None, 'tensor'), may hold values from 0.099609375 to 1.8984375
- norm_bias: bfloat16 [3, 2, 768], P(None, None, 'tensor'), may hold values from -3 to 3
- image_upstream: bfloat16 [16, 197, 768], P('dp', None, 'tensor'), may hold values from -6 to 6
- text_upstream: bfloat16 [8, 512, 768], P('dp', None, 'tensor'), may hold values from -6 to 6
- pair_upstream: bfloat16 [8, 711, 768], P('dp', None, 'tensor'), may hold values from -6 to 6
Outputs:
- image_out: bfloat16 [16, 197, 768], P('dp', None, 'tensor')
- text_out: bfloat16 [8, 512, 768], P('dp', None, 'tensor')
- pair_out: bfloat16 [8, 711, 768], P('dp', None, 'tensor')
- image_input_grad: bfloat16 [16, 197, 768], P('dp', None, 'tensor')
- text_input_grad: bfloat16 [8, 512, 768], P('dp', None, 'tensor')
- pair_input_grad: bfloat16 [8, 711, 768], P('dp', None, 'tensor')
- qkv_grad: float32 [3, 768, 3, 768], P(None, 'dp', None, 'tensor')
- qv_bias_grad: float32 [3, 2, 768], P(None, None, 'tensor')
- out_weight_grad: float32 [3, 768, 768], P(None, 'tensor', 'dp')
- out_bias_grad: float32 [3, 768], P(None, 'tensor')
- up_weight_grad: float32 [3, 768, 3072], P(None, 'dp', 'tensor')
- up_bias_grad: float32 [3, 3072], P(None, 'tensor')
- down_weight_grad: float32 [3, 3072, 768], P(None, 'tensor', 'dp')
- down_bias_grad: float32 [3, 768], P(None, 'tensor')
- norm_gain_grad: float32 [3, 2, 768], P(None, None, 'tensor')
- norm_bias_grad: float32 [3, 2, 768], P(None, None, 'tensor')
Inputs may be any that keep to these rules, and one draw needn't show every extreme that they name: Each text example's first text_lengths rows of 512 are valid; some example of every draw has all 512. Each pair's text rows after its 197 image rows: the first pair_lengths are valid, the rest and the two pad rows are not; some pair of every draw has all 512.
All inputs are finite; a program needn't handle non-finite values.
Results may differ from a plain program's by a relative error of at most 0.017.
Values may be sent and summed in bfloat16 or wider, within the bound.
A program may use at most 192 MiB of HBM per device.

v0:
```python
import math

import jax
import jax.numpy as jnp
from jax import lax
from jax.sharding import PartitionSpec as P

HEAD_DIM = 64
PATCHES = 196


EPSILON = 1e-06


def rounded(value):
    return lax.optimization_barrier(value.astype(jnp.bfloat16)).astype(jnp.float32)


def moments(total_count, square, feature_width):
    mean_val = total_count / feature_width
    return (mean_val, lax.rsqrt(square / feature_width - mean_val * mean_val + EPSILON))


def local_moments(value, feature_width):
    return moments(
        jnp.sum(value, axis=-1, keepdims=True),
        jnp.sum(value * value, axis=-1, keepdims=True),
        feature_width,
    )


def gather_grads(value):
    return lax.all_gather(value, "tensor", axis=2, tiled=True)


def summed_grads(value):
    return lax.psum_scatter(
        rounded(value).astype(jnp.bfloat16), "tensor", scatter_dimension=2, tiled=True
    ).astype(jnp.float32)


def norm_reverse_pass(centered_grad, standardized, inverse_deviation, feature_width):
    total_count, cross_term = lax.psum(
        (
            jnp.sum(centered_grad, axis=-1, keepdims=True),
            jnp.sum(centered_grad * standardized, axis=-1, keepdims=True),
        ),
        "tensor",
    )
    return inverse_deviation * (
        centered_grad - total_count / feature_width - standardized * cross_term / feature_width
    )


def gelu_exact(value):
    return jax.nn.gelu(value, approximate=False)


def masked_scores(queries, key_heads, key_mask, scale):
    scores = (
        jnp.einsum("elhd,emhd->ehlm", queries, key_heads, preferred_element_type=jnp.float32)
        * scale
    )
    return jnp.where(key_mask[:, None, None, :], scores, -1000000000.0)


def forward_tower(row_block, key_mask, weights, tensor_index):
    qkv_w, qv_b, out_w, out_b, up_w, up_b, down_w, down_b, gain, shift = weights
    feature_width = qkv_w.shape[0]
    share = out_w.shape[0]
    examples = row_block.shape[0]
    length = row_block.shape[1]
    head_count = share // HEAD_DIM
    scale = 1.0 / math.sqrt(HEAD_DIM)
    rows_float = row_block.astype(jnp.float32)
    whole_rows, whole_bias, whole_gain, whole_shift = (
        lax.all_gather(row_block, "tensor", axis=2, tiled=True),
        lax.all_gather(out_b, "tensor", axis=0, tiled=True),
        lax.all_gather(gain, "tensor", axis=1, tiled=True),
        lax.all_gather(shift, "tensor", axis=1, tiled=True),
    )
    whole_f = whole_rows.astype(jnp.float32)
    input_mean, input_inverse_deviation = local_moments(whole_f, feature_width)
    normed = (
        (whole_f - input_mean) * input_inverse_deviation * whole_gain[0].astype(jnp.float32)
        + whole_shift[0].astype(jnp.float32)
    ).astype(jnp.bfloat16)
    projected = jnp.einsum("eld,dcf->elcf", normed, qkv_w, preferred_element_type=jnp.float32)
    queries = (
        (projected[:, :, 0] + qv_b[0].astype(jnp.float32))
        .astype(jnp.bfloat16)
        .reshape(examples, length, head_count, HEAD_DIM)
    )
    key_heads = (
        projected[:, :, 1].astype(jnp.bfloat16).reshape(examples, length, head_count, HEAD_DIM)
    )
    value_heads = (
        (projected[:, :, 2] + qv_b[1].astype(jnp.float32))
        .astype(jnp.bfloat16)
        .reshape(examples, length, head_count, HEAD_DIM)
    )
    scores = masked_scores(queries, key_heads, key_mask, scale)
    top_score = jnp.max(scores, axis=-1, keepdims=True)
    log_total = top_score + jnp.log(jnp.sum(jnp.exp(scores - top_score), axis=-1, keepdims=True))
    probs_low = jnp.exp(scores - log_total).astype(jnp.bfloat16)
    mixed = (
        jnp.einsum("ehlm,emhd->elhd", probs_low, value_heads, preferred_element_type=jnp.float32)
        .astype(jnp.bfloat16)
        .reshape(examples, length, share)
    )
    partial_value = jnp.einsum("elf,fd->eld", mixed, out_w, preferred_element_type=jnp.float32)
    attn_full = lax.psum(rounded(partial_value).astype(jnp.bfloat16), "tensor").astype(
        jnp.float32
    ) + whole_bias.astype(jnp.float32)
    resid_full = whole_f + attn_full
    middle_mean, middle_inverse_deviation = local_moments(resid_full, feature_width)
    normed_two = (
        (resid_full - middle_mean) * middle_inverse_deviation * whole_gain[1].astype(jnp.float32)
        + whole_shift[1].astype(jnp.float32)
    ).astype(jnp.bfloat16)
    attention = lax.dynamic_slice_in_dim(attn_full, tensor_index * share, share, 2)
    residual_stream = rows_float + attention
    hidden = jnp.einsum(
        "eld,df->elf", normed_two, up_w, preferred_element_type=jnp.float32
    ) + up_b.astype(jnp.float32)
    activated = gelu_exact(hidden).astype(jnp.bfloat16)
    down_part = jnp.einsum("elf,fd->eld", activated, down_w, preferred_element_type=jnp.float32)
    feedforward = lax.psum_scatter(
        rounded(down_part).astype(jnp.bfloat16), "tensor", scatter_dimension=2, tiled=True
    ).astype(jnp.float32) + down_b.astype(jnp.float32)
    output = residual_stream + feedforward
    kept = (
        normed,
        queries,
        key_heads,
        value_heads,
        log_total,
        mixed,
        normed_two,
        hidden,
        activated,
        input_mean,
        input_inverse_deviation,
        middle_mean,
        middle_inverse_deviation,
        residual_stream,
        rows_float,
    )
    return (output, kept)


def backward_tower(upstream, weights, kept, key_mask):
    qkv_w, qv_b, out_w, out_b, up_w, up_b, down_w, down_b, gain, shift = weights
    (
        normed,
        queries,
        key_heads,
        value_heads,
        log_total,
        mixed,
        normed_two,
        hidden,
        activated,
        input_mean,
        input_inverse_deviation,
        middle_mean,
        middle_inverse_deviation,
        residual_stream,
        rows_float,
    ) = kept
    feature_width = qkv_w.shape[0]
    share = out_w.shape[0]
    examples = queries.shape[0]
    length = queries.shape[1]
    head_count = share // HEAD_DIM
    scale = 1.0 / math.sqrt(HEAD_DIM)
    gain_float = gain.astype(jnp.float32)
    output_gradient = upstream.astype(jnp.float32)
    grad_ffn = output_gradient.astype(jnp.bfloat16)
    down_bias_grad = jnp.sum(grad_ffn, axis=(0, 1), dtype=jnp.float32)
    ffn_full = gather_grads(grad_ffn)
    down_grad = jnp.einsum("elf,eld->fd", activated, ffn_full, preferred_element_type=jnp.float32)
    grad_act = jnp.einsum("eld,fd->elf", ffn_full, down_w, preferred_element_type=jnp.float32)
    grad_hidden = jax.vjp(gelu_exact, hidden)[1](grad_act)[0].astype(jnp.bfloat16)
    up_bias_grad = jnp.sum(grad_hidden, axis=(0, 1), dtype=jnp.float32)
    up_grad = jnp.einsum("eld,elf->df", normed_two, grad_hidden, preferred_element_type=jnp.float32)
    second_normed_gradient = summed_grads(
        jnp.einsum("elf,df->eld", grad_hidden, up_w, preferred_element_type=jnp.float32)
    )
    standardized_middle = (residual_stream - middle_mean) * middle_inverse_deviation
    middle_gain_grad = jnp.sum(second_normed_gradient * standardized_middle, axis=(0, 1))
    shift_mid_grad = jnp.sum(second_normed_gradient, axis=(0, 1))
    residual_gradient = output_gradient + norm_reverse_pass(
        second_normed_gradient * gain_float[1],
        standardized_middle,
        middle_inverse_deviation,
        feature_width,
    )
    grad_attn = residual_gradient.astype(jnp.bfloat16)
    out_bias_grad = jnp.sum(grad_attn, axis=(0, 1), dtype=jnp.float32)
    attn_full = gather_grads(grad_attn)
    out_grad = jnp.einsum("elf,eld->fd", mixed, attn_full, preferred_element_type=jnp.float32)
    grad_mixed = (
        jnp.einsum("eld,fd->elf", attn_full, out_w, preferred_element_type=jnp.float32)
        .astype(jnp.bfloat16)
        .reshape(examples, length, head_count, HEAD_DIM)
    )
    scores = masked_scores(queries, key_heads, key_mask, scale)
    probs_f = jnp.exp(scores - log_total)
    probs_low = probs_f.astype(jnp.bfloat16)
    grad_values = jnp.einsum(
        "ehlm,elhd->emhd", probs_low, grad_mixed, preferred_element_type=jnp.float32
    ).astype(jnp.bfloat16)
    grad_probs = jnp.einsum(
        "elhd,emhd->ehlm", grad_mixed, value_heads, preferred_element_type=jnp.float32
    )
    grad_scores = (
        probs_f * (grad_probs - jnp.sum(probs_f * grad_probs, axis=-1, keepdims=True))
    ).astype(jnp.bfloat16)
    grad_queries = (
        jnp.einsum("ehlm,emhd->elhd", grad_scores, key_heads, preferred_element_type=jnp.float32)
        * scale
    ).astype(jnp.bfloat16)
    grad_keys = (
        jnp.einsum("ehlm,elhd->emhd", grad_scores, queries, preferred_element_type=jnp.float32)
        * scale
    ).astype(jnp.bfloat16)
    grad_qkv = jnp.stack([grad_queries, grad_keys, grad_values], 2).reshape(
        examples, length, 3, share
    )
    qv_bias_grad = jnp.stack(
        [
            jnp.sum(grad_qkv[:, :, 0], axis=(0, 1), dtype=jnp.float32),
            jnp.sum(grad_qkv[:, :, 2], axis=(0, 1), dtype=jnp.float32),
        ],
        0,
    )
    qkv_grad = jnp.einsum("eld,elcf->dcf", normed, grad_qkv, preferred_element_type=jnp.float32)
    normed_gradient = summed_grads(
        jnp.einsum("elcf,dcf->eld", grad_qkv, qkv_w, preferred_element_type=jnp.float32)
    )
    standardized_input = (rows_float - input_mean) * input_inverse_deviation
    input_gain_grad = jnp.sum(normed_gradient * standardized_input, axis=(0, 1))
    shift_in_grad = jnp.sum(normed_gradient, axis=(0, 1))
    grad_input = (
        residual_gradient
        + norm_reverse_pass(
            normed_gradient * gain_float[0],
            standardized_input,
            input_inverse_deviation,
            feature_width,
        )
    ).astype(jnp.bfloat16)
    small_grads = jnp.concatenate(
        [
            qv_bias_grad,
            out_bias_grad[None],
            up_bias_grad.reshape(-1, share),
            down_bias_grad[None],
            jnp.stack([input_gain_grad, middle_gain_grad], 0),
            jnp.stack([shift_in_grad, shift_mid_grad], 0),
        ],
        0,
    )
    return (grad_input, (qkv_grad, out_grad, up_grad, down_grad, small_grads))


def per_device(
    image_rows,
    text_rows,
    pair_rows,
    text_lengths,
    pair_lengths,
    qkv_weight,
    qv_bias,
    out_weight,
    out_bias,
    up_weight,
    up_bias,
    down_weight,
    down_bias,
    norm_gain,
    norm_bias,
    image_upstream,
    text_upstream,
    pair_upstream,
):
    tensor_index = lax.axis_index("tensor")
    image_mask = jnp.ones((image_rows.shape[0], image_rows.shape[1]), dtype=bool)
    text_mask = jnp.arange(text_rows.shape[1], dtype=jnp.int32)[None, :] < text_lengths[:, None]
    pair_mask = jnp.arange(pair_rows.shape[1], dtype=jnp.int32)[None, :] < pair_lengths[:, None] + (
        PATCHES + 1
    )
    towers_in = (
        (image_rows, image_mask, image_upstream),
        (text_rows, text_mask, text_upstream),
        (pair_rows, pair_mask, pair_upstream),
    )
    params = (
        qkv_weight,
        qv_bias,
        out_weight,
        out_bias,
        up_weight,
        up_bias,
        down_weight,
        down_bias,
        norm_gain,
        norm_bias,
    )
    outputs = []
    input_grads = []
    grad_lists = ([], [], [], [], [])
    for tower_id in range(3):
        row_block, key_mask, upstream = towers_in[tower_id]
        weights = tuple((entry[tower_id] for entry in params))
        output, kept = forward_tower(row_block, key_mask, weights, tensor_index)
        outputs.append(output.astype(jnp.bfloat16))
        grad_input, grads = backward_tower(upstream, weights, kept, key_mask)
        input_grads.append(grad_input)
        for slot_id in range(5):
            grad_lists[slot_id].append(grads[slot_id])
    stacked = tuple((jnp.stack(group_list, 0) for group_list in grad_lists))
    qkv_grad, out_weight_grad, up_weight_grad, down_weight_grad = (
        lax.psum_scatter(stacked[0], "dp", scatter_dimension=1, tiled=True),
        lax.psum_scatter(stacked[1], "dp", scatter_dimension=2, tiled=True),
        lax.psum_scatter(stacked[2], "dp", scatter_dimension=1, tiled=True),
        lax.psum_scatter(stacked[3], "dp", scatter_dimension=2, tiled=True),
    )
    small_grads = lax.psum(stacked[4], "dp")
    share = out_weight.shape[1]
    hidden_share = up_weight.shape[2]
    ratio = hidden_share // share
    qv_bias_grad = small_grads[:, 0:2]
    out_bias_grad = small_grads[:, 2]
    up_bias_grad = small_grads[:, 3 : 3 + ratio].reshape(3, hidden_share)
    down_bias_grad = small_grads[:, 3 + ratio]
    norm_gain_grad = small_grads[:, 4 + ratio : 6 + ratio]
    norm_bias_grad = small_grads[:, 6 + ratio : 8 + ratio]
    return (
        outputs[0],
        outputs[1],
        outputs[2],
        input_grads[0],
        input_grads[1],
        input_grads[2],
        qkv_grad,
        qv_bias_grad,
        out_weight_grad,
        out_bias_grad,
        up_weight_grad,
        up_bias_grad,
        down_weight_grad,
        down_bias_grad,
        norm_gain_grad,
        norm_bias_grad,
    )


def solution(mesh):
    return jax.shard_map(
        per_device,
        mesh=mesh,
        in_specs=(
            P("dp", None, "tensor"),
            P("dp", None, "tensor"),
            P("dp", None, "tensor"),
            P("dp"),
            P("dp"),
            P(None, None, None, "tensor"),
            P(None, None, "tensor"),
            P(None, "tensor", None),
            P(None, "tensor"),
            P(None, None, "tensor"),
            P(None, "tensor"),
            P(None, "tensor", None),
            P(None, "tensor"),
            P(None, None, "tensor"),
            P(None, None, "tensor"),
            P("dp", None, "tensor"),
            P("dp", None, "tensor"),
            P("dp", None, "tensor"),
        ),
        out_specs=(
            P("dp", None, "tensor"),
            P("dp", None, "tensor"),
            P("dp", None, "tensor"),
            P("dp", None, "tensor"),
            P("dp", None, "tensor"),
            P("dp", None, "tensor"),
            P(None, "dp", None, "tensor"),
            P(None, None, "tensor"),
            P(None, "tensor", "dp"),
            P(None, "tensor"),
            P(None, "dp", "tensor"),
            P(None, "tensor"),
            P(None, "tensor", "dp"),
            P(None, "tensor"),
            P(None, None, "tensor"),
            P(None, None, "tensor"),
        ),
        check_vma=False,
    )
```

profile of v0, /device:TPU:0, one launch (start us, length us, event | category | flops | bytes accessed | tf_op | source)
XLA Modules:
  0.0 1013.8 jit_solution(11684703509112066378)
XLA Ops:
  8.7 7.9 all-gather.1
  16.7 5.3 fusion.178
  23.4 6.6 all-gather
  30.0 5.3 fusion.179
  35.5 8.7 all_gather.54
  56.0 12.7 %all_gather.58 = bf16[1,512,768]{1,2,0:T(8,128)(2,1)S(1)} all-gather(bf16[1,512,192]{1,2,0:T(8,128)(2,1)S(1)} %copy-done.81), channel_id=1, replica_groups=mesh['dp'=8,'tensor'=4] {'tensor'}, dimensions={2}, use_global_device_ids=true | all-gather | bytes 983040 | tf_op jit(solution)/shard_map/all_gather | solution.py:77
  69.1 6.6 all-gather.4
  75.7 5.3 fusion.174
  81.2 8.3 all-gather.3
  89.5 5.3 fusion.175
  100.3 8.5 all-reduce.8
  123.0 6.1 all-gather.7
  129.1 4.7 fusion.170
  134.1 6.6 all-gather.6
  140.6 4.7 fusion.171
  145.6 9.7 all_gather.66
  160.6 3.6 multiply_convert_fusion.5
  164.2 2.9 convert_reduce_fusion.5
  170.7 3.0 copy.174
  192.4 10.4 %all_gather.68 = bf16[1,512,768]{1,2,0:T(8,128)(2,1)} all-gather(bf16[1,512,192]{1,2,0:T(8,128)(2,1)S(1)} %copy-done.82), channel_id=1, replica_groups=mesh['dp'=8,'tensor'=4] {'tensor'}, dimensions={2}, use_global_device_ids=true | all-gather | bytes 983040 | tf_op jit(solution)/shard_map/all_gather | solution.py:33
  202.8 51.7 %all-reduce.19.cloned.1.call-done = (bf16[1,512,768]{2,1,0:T(8,128)(2,1)}, bf16[1,711,768]{2,1,0:T(8,128)(2,1)}, bf16[2,197,768]{1,0,2:T(2,128)(2,1)}) async-done(((bf16[1,512,768]{2,1,0:T(8,128)(2,1)}, bf16[1,711,768]{2,1,0:T(8,128)(2,1)}, bf16[2,197,768]{1,0,2:T(2,128)(2,1)}), (bf16[1,512,768]{2,1,0:T(8,128)(2,1)}, bf16[1,711,768]{2,1,0:T(8,128)(2,1)}, ...) | async-done | bytes 2483728 | tf_op jit(solution)/shard_map/psum | solution.py:112
  254.5 3.0 fusion.133
  257.6 6.4 multiply_convert_fusion.3
  264.0 3.1 convert_reduce_fusion.4
  268.0 3.0 fusion.34
  270.9 4.7 copy.225
  278.3 3.2 fusion.33
  281.4 4.8 copy.221
  290.8 9.1 multiply_convert_fusion.2
  300.0 5.4 convert_reduce_fusion.2
  306.3 3.3 fusion.28
  309.7 6.7 copy.229
  316.3 2.9 copy.269
  332.7 4.5 slice_reduce_fusion.4
  337.3 4.5 slice_reduce_fusion.2
  341.8 4.5 slice_reduce_fusion
  346.9 2.9 convolution_convert_fusion.7
  349.8 3.0 copy.161
  356.3 3.6 fusion.27
  360.0 6.7 copy.223
  366.6 2.9 copy.270
  389.3 11.8 %all-reduce.7 = (f32[2,197]{1,0:T(2,128)}, f32[2,197,1]{1,0,2:T(2,128)}, f32[512]{0:T(512)}, f32[1,512,1]{1,2,0:T(1,128)}, f32[711]{0:T(1024)}, /*index=5*/f32[1,711,1]{1,2,0:T(1,128)}) all-reduce(f32[2,197]{1,0:T(2,128)} %get-tuple-element.87, f32[2,197,1]{1,0,2:T(2,128)} %bitcast.503, ...), channel_id=1, replica_groups=mesh['dp'=8,'tensor'=4] {'tensor'}, use_global_device_ids=true, to_apply=%region_28.29 | all-reduce | flops 3234 | bytes 25872 | tf_op jit(solution)/shard_map/psum | solution.py:43
  401.8 3.0 convert_reduce_fusion.19
  406.5 8.9 all_gather.67
  424.6 3.0 copy.184
  427.7 3.6 convert_reduce_fusion.17
  437.8 4.1 convert_reduce_fusion.11
  443.8 9.1 all_gather.69
  464.6 2.9 copy.227
  473.5 5.3 multiply_reduce_fusion
  486.1 2.8 copy.231
  493.8 3.0 copy.235
  496.8 2.8 reshape.1243
  504.6 3.3 pad_maximum_fusion.1
  507.9 10.9 %copy.237 = f32[3,768,768]{1,0,2:T(4,128)} copy(f32[3,768,768]{2,1,0:T(8,128)} %pad_maximum_fusion.1) | data formatting | bytes 14155776
  518.8 8.2 copy.255
  535.9 9.8 copy.233
  545.7 11.3 %reshape.1241 = f32[768,1728]{1,0:T(8,128)} reshape(f32[768,3,3,192]{3,2,1,0:T(4,128)} %bitcast.422) | data formatting | bytes 10616832
  563.3 3.4 pad_maximum_fusion
  577.8 10.9 %all-reduce.6 = (f32[2,197]{1,0:T(2,128)S(1)}, f32[2,197,1]{1,0,2:T(2,128)S(1)}, f32[512]{0:T(512)S(1)}, f32[1,512,1]{1,2,0:T(1,128)S(1)}, f32[711]{0:T(1024)S(1)}, /*index=5*/f32[1,711,1]{1,2,0:T(1,128)S(1)}) all-reduce(f32[2,197]{1,0:T(2,128)S(1)} %get-tuple-element.105, ...), channel_id=1, replica_groups=mesh['dp'=8,'tensor'=4] {'tensor'}, use_global_device_ids=true, to_apply=%region_34.35 | all-reduce | flops 3234 | bytes 25872 | tf_op jit(solution)/shard_map/psum | solution.py:43
  597.6 38.3 %psum.127 = f32[3,12,192]{2,1,0:T(8,128)S(1)} all-reduce(f32[3,12,192]{2,1,0:T(8,128)S(1)} %pad_maximum_fusion.9), channel_id=1, replica_groups=mesh['dp'=8,'tensor'=4] {'dp'}, use_global_device_ids=true, to_apply=%region_85.86 | all-reduce | flops 6912 | bytes 55296 | tf_op jit(solution)/shard_map/psum | solution.py:330
  639.9 125.0 %reduce-scatter.47.cloned.1.call-done = f32[96,2304]{1,0:T(8,128)} async-done(((f32[768,2304]{1,0:T(8,128)}), f32[96,2304]{1,0:T(8,128)}) %reduce-scatter.47.cloned.1.call-update) | async-done | bytes 884752
  767.6 106.9 %reduce-scatter.43.cloned.1.call-done = f32[96,1728]{1,0:T(8,128)} async-done(((f32[768,1728]{1,0:T(8,128)}), f32[96,1728]{1,0:T(8,128)}) %reduce-scatter.43.cloned.1.call-update) | async-done | bytes 663568
  877.3 129.8 %reduce-scatter.29.cloned.1.call-done = f32[3,96,768]{2,1,0:T(8,128)} async-done(((f32[3,768,768]{2,1,0:T(8,128)}), f32[3,96,768]{2,1,0:T(8,128)}) %reduce-scatter.29.cloned.1.call-update) | async-done | bytes 884752 | tf_op jit(solution)/shard_map/reduce_scatter | solution.py:327
  (684 shorter events, 204.2 us)
Async XLA Ops:
  7.2 28.1 %copy-start.77 = (bf16[2,197,192]{1,2,0:T(8,128)(2,1)S(1)}, bf16[2,197,192]{1,2,0:T(8,128)(2,1)}, u32[]{:S(2)}) copy-start(bf16[2,197,192]{1,2,0:T(8,128)(2,1)} %param.18) | copy-start | bytes 453892
  7.2 148.1 %all-reduce.15.cloned.1.call-start = ((), (), s32[]{:S(2)}) async-start(), calls=%async_computation.10 | async-start | bytes 1228800 | tf_op jit(solution)/shard_map/psum | solution.py:112
  22.0 23.2 %copy-start.166 = (f32[768]{0:T(1024)}, f32[768]{0:T(1024)S(1)}, u32[]{:S(2)}) copy-start(f32[768]{0:T(1024)S(1)} %get-tuple-element.116) | copy-start | bytes 9220
  23.4 12.1 %copy-start.66 = (bf16[1,2,192]{1,0,2:T(2,128)(2,1)}, bf16[1,2,192]{1,0,2:T(2,128)(2,1)S(1)}, u32[]{:S(2)}) copy-start(bf16[1,2,192]{1,0,2:T(2,128)(2,1)S(1)} %copy.249) | copy-start | bytes 2308
  35.3 9.8 copy-start.168
  52.7 121.1 %all-gather.13.cloned.1.call-start = ((), (), s32[]{:S(2)}) async-start(), calls=%async_computation.11 | async-start | bytes 1474560 | tf_op jit(solution)/shard_map/all_gather | solution.py:77
  53.4 201.1 %all-reduce.19.cloned.1.call-start = ((), (), s32[]{:S(2)}) async-start(), calls=%async_computation.25 | async-start | bytes 5332992 | tf_op jit(solution)/shard_map/psum | solution.py:112
  69.0 26.1 %copy-start.11 = (bf16[1,512,768]{2,1,0:T(8,128)(2,1)}, bf16[1,512,768]{2,1,0:T(8,128)(2,1)S(1)}, u32[]{:S(2)}) copy-start(bf16[1,512,768]{2,1,0:T(8,128)(2,1)S(1)} %copy.164) | copy-start | bytes 2359300
  81.0 15.0 %copy-start.174 = (f32[768]{0:T(1024)}, f32[768]{0:T(1024)S(1)}, u32[]{:S(2)}) copy-start(f32[768]{0:T(1024)S(1)} %get-tuple-element.112) | copy-start | bytes 9220
  81.2 14.8 %copy-start.68 = (bf16[1,2,192]{1,0,2:T(2,128)(2,1)}, bf16[1,2,192]{1,0,2:T(2,128)(2,1)S(1)}, u32[]{:S(2)}) copy-start(bf16[1,2,192]{1,0,2:T(2,128)(2,1)S(1)} %copy.251) | copy-start | bytes 2308
  97.6 14.4 %copy-start.25 = (f32[1,512,1,192]{1,3,2,0:T(8,128)}, f32[1,512,1,192]{1,3,2,0:T(8,128)S(1)}, u32[]{:S(2)}) copy-start(f32[1,512,1,192]{1,3,2,0:T(8,128)S(1)} %get-tuple-element.191) | copy-start | bytes 1179652
  118.5 15.4 %copy-start.199 = (bf16[1,2,192]{2,1,0:T(2,128)(2,1)S(1)}, bf16[1,2,192]{2,1,0:T(2,128)(2,1)}, u32[]{:S(2)}) copy-start(bf16[1,2,192]{2,1,0:T(2,128)(2,1)} %get-tuple-element.209) | copy-start | bytes 2308
  121.4 24.0 %copy-start.203 = (f32[192]{0:T(256)S(1)}, f32[192]{0:T(256)}, u32[]{:S(2)}) copy-start(f32[192]{0:T(256)} %get-tuple-element.144) | copy-start | bytes 2308
  121.4 24.1 %copy-start.202 = (f32[192]{0:T(256)S(1)}, f32[192]{0:T(256)}, u32[]{:S(2)}) copy-start(f32[192]{0:T(256)} %get-tuple-element.139) | copy-start | bytes 2308
  121.4 24.1 %copy-start.83 = (bf16[2,197,192]{1,2,0:T(8,128)(2,1)S(1)}, bf16[2,197,192]{1,2,0:T(8,128)(2,1)}, u32[]{:S(2)}) copy-start(bf16[2,197,192]{1,2,0:T(8,128)(2,1)} %param.33) | copy-start | bytes 453892
  122.2 61.6 %copy-start.110 = (pred[711]{0:T(1024)(128)(4,1)}, pred[711]{0:T(1024)(128)(4,1)S(1)}, u32[]{:S(2)}) copy-start(pred[711]{0:T(1024)(128)(4,1)S(1)} %iota_compare_fusion) | copy-start | bytes 2137
  129.1 26.2 %copy-start.140 = (f32[768]{0:T(1024)S(1)}, f32[768]{0:T(1024)}, u32[]{:S(2)}) copy-start(f32[768]{0:T(1024)} %convert_element_type.887) | copy-start | bytes 9220
  133.9 44.0 %copy-start.182 = (f32[768]{0:T(1024)}, f32[768]{0:T(1024)S(1)}, u32[]{:S(2)}) copy-start(f32[768]{0:T(1024)S(1)} %get-tuple-element.108) | copy-start | bytes 9220
  133.9 156.9 %copy-start.178 = (f32[768]{0:T(1024)}, f32[768]{0:T(1024)S(1)}, u32[]{:S(2)}) copy-start(f32[768]{0:T(1024)S(1)} %get-tuple-element.109) | copy-start | bytes 9220
  134.1 23.9 %copy-start.70 = (bf16[1,2,192]{1,0,2:T(2,128)(2,1)}, bf16[1,2,192]{1,0,2:T(2,128)(2,1)S(1)}, u32[]{:S(2)}) copy-start(bf16[1,2,192]{1,0,2:T(2,128)(2,1)S(1)} %copy.253) | copy-start | bytes 2308
  145.4 32.4 %copy-start.184 = (f32[768]{0:T(1024)}, f32[768]{0:T(1024)S(1)}, u32[]{:S(2)}) copy-start(f32[768]{0:T(1024)S(1)} %get-tuple-element.106) | copy-start | bytes 9220
  145.4 145.4 %copy-start.180 = (f32[768]{0:T(1024)}, f32[768]{0:T(1024)S(1)}, u32[]{:S(2)}) copy-start(f32[768]{0:T(1024)S(1)} %get-tuple-element.107) | copy-start | bytes 9220
  145.5 35.2 %copy-start.134 = (f32[3,64]{1,0:T(4,128)}, f32[3,64]{1,0:T(4,128)S(1)}, u32[]{:S(2)}) copy-start(f32[3,64]{1,0:T(4,128)S(1)} %reshape.1120) | copy-start | bytes 2308
  145.6 40.9 %copy-start.136 = (f32[3,64]{1,0:T(4,128)}, f32[3,64]{1,0:T(4,128)S(1)}, u32[]{:S(2)}) copy-start(f32[3,64]{1,0:T(4,128)S(1)} %reshape.1119) | copy-start | bytes 2308
  145.6 12.4 %copy-start.162 = (f32[768]{0:T(1024)S(1)}, f32[768]{0:T(1024)}, u32[]{:S(2)}) copy-start(f32[768]{0:T(1024)} %get-tuple-element.117) | copy-start | bytes 9220
  145.6 12.4 %copy-start.164 = (f32[768]{0:T(1024)S(1)}, f32[768]{0:T(1024)}, u32[]{:S(2)}) copy-start(f32[768]{0:T(1024)} %get-tuple-element.115) | copy-start | bytes 9220
  145.6 12.4 %copy-start.209 = (f32[768]{0:T(1024)S(1)}, f32[768]{0:T(1024)}, u32[]{:S(2)}) copy-start(f32[768]{0:T(1024)} %get-tuple-element.137) | copy-start | bytes 9220
  191.5 108.5 %all-gather.15.cloned.1.call-start = ((), (), s32[]{:S(2)}) async-start(), calls=%async_computation.12 | async-start | bytes 1474560 | tf_op jit(solution)/shard_map/all_gather | solution.py:33
  192.1 179.9 %reduce-scatter.35.cloned.1.call-start = ((), (), s32[]{:S(2)}) async-start(), calls=%async_computation.17 | async-start | bytes 983040
  192.4 65.1 %copy-start.142 = (f32[768]{0:T(1024)}, f32[768]{0:T(1024)S(1)}, u32[]{:S(2)}) copy-start(f32[768]{0:T(1024)S(1)} %convert_element_type.888) | copy-start | bytes 9220
  278.2 97.5 %reduce-scatter.31.cloned.1.call-start = ((), (), s32[]{:S(2)}) async-start(), calls=%async_computation.15 | async-start | bytes 983040
  278.3 12.6 %copy-start.144 = (f32[768]{0:T(1024)}, f32[768]{0:T(1024)S(1)}, u32[]{:S(2)}) copy-start(f32[768]{0:T(1024)S(1)} %convert_element_type.889) | copy-start | bytes 9220
  290.7 9.2 copy-start.98
  290.7 9.2 copy-start.101
  290.7 91.2 %reduce-scatter.39.cloned.1.call-start = ((), (), s32[]{:S(2)}) async-start(), calls=%async_computation.19 | async-start | bytes 1474560
  319.3 114.4 %reduce-scatter.33.cloned.1.call-start = ((), (), s32[]{:S(2)}) async-start(), calls=%async_computation.16 | async-start | bytes 1474560
  323.0 23.3 %copy-start.161 = (bf16[3,192]{1,0:T(4,128)(2,1)S(1)}, bf16[3,192]{1,0:T(4,128)(2,1)}, u32[]{:S(2)}) copy-start(bf16[3,192]{1,0:T(4,128)(2,1)} %param.30) | copy-start | bytes 3460
  324.9 112.9 %copy-start.9 = (bf16[1,711,192]{2,1,0:T(8,128)(2,1)}, bf16[1,711,192]{2,1,0:T(8,128)(2,1)S(1)}, u32[]{:S(2)}) copy-start(bf16[1,711,192]{2,1,0:T(8,128)(2,1)S(1)} %copy.168) | copy-start | bytes 819076
  337.3 32.3 %copy-start.138 = (f32[192]{0:T(256)}, f32[192]{0:T(256)S(1)}, u32[]{:S(2)}) copy-start(f32[192]{0:T(256)S(1)} %get-tuple-element.135) | copy-start | bytes 2308
  369.5 100.9 %all-gather.17.cloned.1.call-start = ((), (), s32[]{:S(2)}) async-start(), calls=%async_computation.13 | async-start | bytes 1474560 | tf_op jit(solution)/shard_map/all_gather | solution.py:33
  369.6 9.8 copy-start.128
  369.6 9.8 copy-start.131
  372.0 7.5 copy-start.153
  401.7 15.1 %copy-start.121 = (f32[2,197]{1,0:T(2,128)}, f32[2,197]{1,0:T(2,128)S(1)}, u32[]{:S(2)}) copy-start(f32[2,197]{1,0:T(2,128)S(1)} %multiply_bitcast_fusion.1) | copy-start | bytes 4732
  406.5 10.4 %copy-start.2 = (f32[2,3,197,197]{2,3,1,0:T(8,128)S(1)}, f32[2,3,197,197]{2,3,1,0:T(8,128)}, u32[]{:S(2)}) copy-start(f32[2,3,197,197]{2,3,1,0:T(8,128)} %copy-done.1) | copy-start | bytes 2794252
  406.5 10.4 %copy-start.32 = (f32[2,197,1,192]{1,3,2,0:T(8,128)S(1)}, f32[2,197,1,192]{1,3,2,0:T(8,128)}, u32[]{:S(2)}) copy-start(f32[2,197,1,192]{1,3,2,0:T(8,128)} %copy-done.31) | copy-start | bytes 907780
  431.2 6.6 copy-start.186
  431.2 6.6 copy-start.200
  443.8 125.9 %all-reduce.17.cloned.1.call-start = ((), (), s32[]{:S(2)}) async-start(), calls=%async_computation.24 | async-start | bytes 3145728
  443.8 11.4 %copy-start.5 = (bf16[3,512,512]{1,2,0:T(8,128)(2,1)S(1)}, bf16[3,512,512]{1,2,0:T(8,128)(2,1)}, u32[]{:S(2)}) copy-start(bf16[3,512,512]{1,2,0:T(8,128)(2,1)} %fusion.14) | copy-start | bytes 4718596
  460.0 112.7 %reduce-scatter.37.cloned.1.call-start = ((), (), s32[]{:S(2)}) async-start(), calls=%async_computation.18 | async-start | bytes 983040
  470.2 104.9 %reduce-scatter.41.cloned.1.call-start = ((), (), s32[]{:S(2)}) async-start(), calls=%async_computation.20 | async-start | bytes 1474560
  473.5 9.7 copy-start.58
  490.3 147.6 %reduce-scatter.45.cloned.1.call-start = ((), (), s32[]{:S(2)}) async-start(), calls=%async_computation.22 | async-start | bytes 2211840
  499.7 265.2 %reduce-scatter.47.cloned.1.call-start = ((), (), s32[]{:S(2)}) async-start(), calls=%async_computation.23 | async-start | bytes 7962624
  527.1 347.3 %reduce-scatter.43.cloned.1.call-start = ((), (), s32[]{:S(2)}) async-start(), calls=%async_computation.21 | async-start | bytes 6193152
  557.1 450.0 %reduce-scatter.29.cloned.1.call-start = ((), (), s32[]{:S(2)}) async-start(), calls=%async_computation.14 | async-start | bytes 7962624 | tf_op jit(solution)/shard_map/reduce_scatter | solution.py:327
  574.3 14.4 %copy-start.35 = (bf16[2,197,192]{2,1,0:T(8,128)(2,1)S(1)}, bf16[2,197,192]{2,1,0:T(8,128)(2,1)}, u32[]{:S(2)}) copy-start(bf16[2,197,192]{2,1,0:T(8,128)(2,1)} %copy.175) | copy-start | bytes 453892
  574.3 14.4 %copy-start.47 = (bf16[2,197,192]{2,1,0:T(8,128)(2,1)S(1)}, bf16[2,197,192]{2,1,0:T(8,128)(2,1)}, u32[]{:S(2)}) copy-start(bf16[2,197,192]{2,1,0:T(8,128)(2,1)} %copy.173) | copy-start | bytes 453892
  574.3 14.4 %copy-start.122 = (f32[2,197]{1,0:T(2,128)S(1)}, f32[2,197]{1,0:T(2,128)}, u32[]{:S(2)}) copy-start(f32[2,197]{1,0:T(2,128)} %copy-done.121) | copy-start | bytes 4732
  574.3 14.4 %copy-start.139 = (f32[192]{0:T(256)S(1)}, f32[192]{0:T(256)}, u32[]{:S(2)}) copy-start(f32[192]{0:T(256)} %copy-done.138) | copy-start | bytes 2308
  574.4 14.4 %copy-start.159 = (f32[2,197]{1,0:T(2,128)S(1)}, f32[2,197]{1,0:T(2,128)}, u32[]{:S(2)}) copy-start(f32[2,197]{1,0:T(2,128)} %get-tuple-element.154) | copy-start | bytes 4732
  574.4 14.4 %copy-start.198 = (f32[1,192]{1,0:T(1,128)S(1)}, f32[1,192]{1,0:T(1,128)}, u32[]{:S(2)}) copy-start(f32[1,192]{1,0:T(1,128)} %get-tuple-element.216) | copy-start | bytes 2308
  577.2 17.8 %copy-start.46 = (f32[1,512,192]{2,1,0:T(8,128)S(1)}, f32[1,512,192]{2,1,0:T(8,128)}, u32[]{:S(2)}) copy-start(f32[1,512,192]{2,1,0:T(8,128)} %get-tuple-element.172) | copy-start | bytes 1179652
  (176 other events, 409.9 us)
Sparse Core Ops, SparseCore 0:
  52.8 36.8 all-reduce.14
  91.3 18.2 all-gather.12
  191.6 62.8 all-reduce.18
  255.9 17.4 all-gather.14
  278.3 23.3 reduce-scatter.34
  304.1 23.2 reduce-scatter.30
  329.9 25.5 reduce-scatter.38
  369.7 25.7 reduce-scatter.32
  443.9 17.4 all-gather.16
  464.8 42.8 all-reduce.16
  510.2 23.2 reduce-scatter.36
  536.0 25.6 reduce-scatter.40
  565.1 67.9 reduce-scatter.44
  636.6 128.2 reduce-scatter.46
  768.3 106.0 reduce-scatter.42
  878.5 128.5 reduce-scatter.28
where the time goes:
time: 1030 us; the launch traced here: 1010 us
  waiting for transfers between devices  415 us (40%)
  local copies, waits for them, and re-layouts  204 us (20%)
  blocking collectives  171 us (17%)
  matrix products  106 us (10%)
  other arithmetic  96.2 us (9%)
  between operations  19.6 us (2%)
    unnamed x26, waiting for transfers between devices  233 us
    unnamed x514, local copies, waits for them, and re-layouts  160 us
    reduce_scatter x1, waiting for transfers between devices, per_device(): lax.psum_scatter(stacked[2], 'dp', scatter_dimension=1, tiled=True)  130 us
    psum x2, waiting for transfers between devices, forward_tower(): lax.psum(rounded(partial_value).astype(jnp.bfloat16), 'tensor')  51.7 us
    psum x1, blocking collectives, per_device(): small_grads = lax.psum(stacked[4], 'dp')  38.3 us
    all_gather x4, blocking collectives, gather_grads(): return lax.all_gather(value, 'tensor', axis=2, tiled=True)  38.1 us
    psum x2, blocking collectives, norm_reverse_pass(): lax.psum((jnp.sum(centered_grad, axis=-1, keepdims=True), jnp.sum(centere...  22.7 us
    all_gather x3, blocking collectives, forward_tower(): lax.all_gather(gain, 'tensor', axis=1, tiled=True)  21.4 us
  transfers between devices with their start and end apart: 16, of which 4 were waited for; matrix products, arithmetic and copies ran while one was open for 34% of the time, Pallas kernels for 0%

commit v1 on v0

v1 whole, which is shorter than its diff:
```python
from types import SimpleNamespace

import jax
import jax.numpy as jnp
from jax import lax
from jax.experimental import pallas as pl
from jax.experimental.pallas import tpu as pltpu
from jax.sharding import PartitionSpec as P

HEAD_DIM = 64
PATCHES = 196
EPSILON = 1e-06
TOWERS = 3
FIRST, SECOND = 0, 1
FFN, ATTN = 0, 1
TILE = 256
COLS = 12
N_REMOTE = 160
BF16 = jnp.bfloat16
F32 = jnp.float32
MESH = pl.DeviceIdType.MESH
INV_SQRT2 = 0.7071067811865476
INV_SQRT_2PI = 0.3989422804014327


def nn(a, b):
    return lax.dot_general(a, b, (((1,), (0,)), ((), ())), preferred_element_type=F32)


def nt(a, b):
    return lax.dot_general(a, b, (((1,), (1,)), ((), ())), preferred_element_type=F32)


def up(value, multiple):
    return -(-value // multiple) * multiple


class Plan:
    def __init__(self, rows, weights, dp, tensor):
        qkv, out, upw = weights
        self.dp = dp
        self.examples = [r.shape[0] for r in rows]
        self.length = [r.shape[1] for r in rows]
        self.padded = [up(n, TILE) for n in self.length]
        self.lanes = [e * n for e, n in zip(self.examples, self.padded)]
        self.width = qkv.shape[1]
        self.share = out.shape[1]
        self.hidden = upw.shape[2]
        self.heads = self.share // HEAD_DIM
        self.grad_lanes = (2 * self.hidden, 4 * self.share)
        self.pad = (3 * self.share) % TILE
        assert tensor == 4 and self.width == 4 * self.share
        assert self.pad + self.share == TILE and self.hidden % TILE == 0
        self.fused = dp % 2 == 0 and dp > 1 and self.width % (16 * dp) == 0
        self.nz = dp // 2 if self.fused else 1
        self.slab = self.width // dp if self.fused else self.width
        self.halves = 2 if self.fused else 1


class Out:
    def __init__(self, spec, shape, dtype=F32):
        self.spec, self.shape, self.dtype = spec, shape, dtype


def flatten(tree):
    return jax.tree.flatten(tree, is_leaf=lambda v: not isinstance(v, (dict, list)))


def scratch(plan):
    width, share, hidden, nz = plan.width, plan.share, plan.hidden, plan.nz
    half, most = width // 2, max(plan.lanes)
    dma = pltpu.SemaphoreType.DMA

    def vm(*shape, dtype=BF16):
        return pltpu.VMEM(shape, dtype)

    def each(*lead, dtype=BF16):
        return [pltpu.VMEM((*lead, lanes), dtype) for lanes in plan.lanes]

    k = SimpleNamespace()
    k.x, k.dy, k.n = each(width), each(width), each(width)
    k.sums = [each(width), each(width)]
    k.part, k.rpart = each(width), each(width)
    k.qkv, k.m = each(3 * share), each(TILE)
    k.p = [vm(e * plan.heads, n, n) for e, n in zip(plan.examples, plan.padded)]
    k.near, k.far = each(half), [each(half), each(half)]
    k.rnear, k.rfar = each(2, share), [each(share), each(share)]
    k.own, k.row = each(share, dtype=F32), each(8, dtype=F32)
    k.stat_own, k.stat_near = each(8, dtype=F32), each(8, dtype=F32)
    k.stat_chip, k.stat_far = each(8, dtype=F32), each(8, dtype=F32)
    land = plan.slab if plan.fused else 16
    k.g_all = [vm(plan.halves, nz, plan.slab, n) for n in plan.grad_lanes]
    k.g_y = [vm(nz, land, n) for n in plan.grad_lanes]
    k.g_z = [vm(nz, land, n) for n in plan.grad_lanes]
    k.credit = [pltpu.SemaphoreType.REGULAR for _ in plan.grad_lanes]
    k.out_sem = [dma((2,)) for _ in plan.grad_lanes]
    if plan.fused:
        k.g_far = [
            [vm(max(nz - 1, 1), plan.slab, n) for _ in range(TOWERS)] for n in plan.grad_lanes
        ]
        k.s_ffn = vm(2, plan.slab, hidden, dtype=F32)
        k.s_qkv = vm(3, plan.slab, share, dtype=F32)
        k.s_out = vm(share, plan.slab, dtype=F32)
    k.wqkv_v, k.wout_v = vm(2, 3 * share, width), vm(2, share, width)
    k.wup_v, k.wdown_v = vm(width, hidden), vm(hidden, width)
    k.up_t, k.down_t = vm(hidden, width), vm(width, hidden)
    k.work_n, k.work_a = vm(width, most), vm(hidden, most)
    k.work_h, k.work_m = vm(width, most), vm(share, most)
    k.pown, k.pfull = vm(share, 128, dtype=F32), vm(width, 128)
    k.small, k.small_y = vm(share, 128, dtype=F32), vm(share, 128, dtype=F32)
    k.small_z = vm(nz, share, 128, dtype=F32)
    k.in_sem, k.w_sem, k.part_sem = dma((2 * TOWERS,)), dma((18,)), dma((TOWERS,))
    k.send_sem, k.recv_sem = dma((N_REMOTE,)), dma((N_REMOTE,))
    return k


def kernel(plan, r):
    width, share, hidden, heads = plan.width, plan.share, plan.hidden, plan.heads
    half = width // 2
    nz = plan.nz

    dp_at = lax.axis_index("dp")
    me = lax.axis_index("tensor")
    core = lax.rem(me, 2)
    chip = lax.div(me, 2)
    y_at = lax.rem(dp_at, 2)
    z_at = lax.div(dp_at, 2)
    sibling = (dp_at, me + 1 - 2 * core)
    across = (dp_at, lax.rem(me + 2, 4))
    y_peer = (dp_at + 1 - 2 * y_at, me)

    def z_index(k):
        return lax.rem(z_at + k, nz)

    def z_peer(k):
        return (z_index(k) * 2 + y_at, me)

    counter = [0]
    pending = []

    def remote(src, dst, device):
        at = counter[0]
        counter[0] += 1
        assert at < N_REMOTE
        return pltpu.make_async_remote_copy(
            src_ref=src,
            dst_ref=dst,
            send_sem=r.send_sem.at[at],
            recv_sem=r.recv_sem.at[at],
            device_id=device,
            device_id_type=MESH,
        )

    def launch(copy):
        copy.start()
        pending.append(copy)
        return copy

    def sent(copy):
        copy.wait_send()
        pending[:] = [other for other in pending if other is not copy]

    def block(at, size):
        return pl.ds(pl.multiple_of(at * size, size), size)

    own = block(me, share)
    my_half, other_half = block(core, half), block(1 - core, half)

    def lanes_loop(lanes, tile, body):
        def step(at, carry):
            body(block(at, tile))
            return carry

        lax.fori_loop(0, lanes // tile, step, 0)

    lane_of_small = lax.broadcasted_iota(jnp.int32, (share, 128), 1)

    def keep_sum(t, j, value):
        column = jnp.sum(value.astype(F32), axis=1, keepdims=True)
        small = r.small
        small[...] = jnp.where(lane_of_small == t * COLS + j, column, small[...])

    def own_col(t, j):
        return r.pown[:, t * COLS + j : t * COLS + j + 1]

    def full_col(t, j):
        return r.pfull[...].astype(F32)[:, t * COLS + j : t * COLS + j + 1]

    class Gather:
        def __init__(self, buf):
            self.to_sibling = remote(buf.at[own], buf.at[own], sibling)
            self.to_across = remote(buf.at[own], buf.at[own], across)
            blk = block(lax.rem(me + 2, 4), share)
            self.forwarded = remote(buf.at[blk], buf.at[blk], sibling)

        def start(self):
            launch(self.to_across)
            launch(self.to_sibling)

        def forward(self):
            self.to_across.wait_recv()
            launch(self.forwarded)

        def finish(self):
            self.to_sibling.wait_recv()
            self.forwarded.wait_recv()

    class AllReduce:
        def __init__(self, t, which):
            self.part, self.near = r.part[t], r.near[t]
            self.far, self.out = r.far[which][t], r.sums[which][t]
            self.c1 = remote(self.part.at[other_half], self.near, sibling)
            self.c2 = remote(self.part.at[my_half], self.far, across)
            self.c3 = remote(self.out.at[my_half], self.out.at[my_half], sibling)

        def begin(self):
            launch(self.c1)

        def cross(self):
            self.c1.wait_recv()
            total = self.part[my_half].astype(F32) + self.near[...].astype(F32)
            self.part[my_half] = total.astype(BF16)
            launch(self.c2)

        def back(self):
            self.c2.wait_recv()
            total = self.part[my_half].astype(F32) + self.far[...].astype(F32)
            self.out[my_half] = total.astype(BF16)
            launch(self.c3)

        def finish(self):
            self.c3.wait_recv()

        def free(self):
            sent(self.c1)
            sent(self.c2)
            sent(self.c3)

    class Scatter:
        def __init__(self, t, which):
            self.part, self.near, self.far = r.rpart[t], r.rnear[t], r.rfar[which][t]
            self.far_blk = block(2 * (1 - chip) + core, share)
            theirs = (2 * (1 - chip) + 1 - core, 2 * chip + 1 - core)
            self.c1 = [
                remote(self.part.at[block(theirs[j], share)], self.near.at[j], sibling)
                for j in range(2)
            ]
            self.c2 = remote(self.part.at[self.far_blk], self.far, across)

        def begin(self):
            for copy in self.c1:
                launch(copy)

        def cross(self):
            self.c1[0].wait_recv()
            blk = self.far_blk
            self.part[blk] = (self.part[blk].astype(F32) + self.near[0].astype(F32)).astype(BF16)
            launch(self.c2)
            self.c1[1].wait_recv()
            self.part[own] = (self.part[own].astype(F32) + self.near[1].astype(F32)).astype(BF16)

        def finish(self):
            self.c2.wait_recv()

        def free(self):
            for copy in self.c1:
                sent(copy)
            sent(self.c2)

    class Stats:
        def __init__(self, t):
            self.c1 = remote(r.stat_own[t], r.stat_near[t], sibling)
            self.c2 = remote(r.stat_chip[t], r.stat_far[t], across)
            self.t = t

        def begin(self):
            launch(self.c1)

        def cross(self):
            t = self.t
            self.c1.wait_recv()
            r.stat_chip[t][...] = r.stat_own[t][...] + r.stat_near[t][...]
            launch(self.c2)

        def finish(self):
            self.c2.wait_recv()

    class GradSum:
        def __init__(self, which):
            self.all, self.land, self.sums = r.g_all[which], r.g_y[which], r.g_z[which]
            self.credit = r.credit[which]
            self.which = which
            self.y_copies, self.z_copies, self.hbm = {}, {}, {}

        def send(self, t):
            if not plan.fused:
                copy = pltpu.make_async_copy(
                    self.all.at[0, 0], r.o_g[self.which].at[t], r.part_sem.at[t]
                )
                copy.start()
                copy.wait()
                return
            if t:
                pl.semaphore_wait(self.credit, 1)
            self.y_copies[t] = []
            for j in range(nz):
                at = z_index(1 + j)
                copy = remote(self.all.at[1 - y_at, at], self.land.at[at], y_peer)
                self.y_copies[t].append(launch(copy))

        def relay(self, t):
            if not plan.fused:
                return
            if t:
                for copy in self.z_copies[t - 1]:
                    sent(copy)
            self.z_copies[t] = []
            for j in range(nz):
                at = z_index(1 + j)
                copy = self.y_copies[t][j]
                copy.wait_recv()
                total = self.all[y_at, at].astype(F32) + self.land[at].astype(F32)
                self.sums[at] = total.astype(BF16)
                if j < nz - 1:
                    dst = r.g_far[self.which][t].at[j]
                    self.z_copies[t].append(launch(remote(self.sums.at[at], dst, z_peer(1 + j))))
            for copy in self.y_copies[t]:
                sent(copy)
            if t < TOWERS - 1:
                pl.semaphore_signal(self.credit, inc=1, device_id=y_peer, device_id_type=MESH)

        def finish(self, t):
            if not plan.fused:
                return
            total = self.sums[z_at].astype(F32)
            for j in range(nz - 1):
                self.z_copies[t][j].wait_recv()
                total = total + r.g_far[self.which][t][j].astype(F32)
            if t:
                for copy in self.hbm[t - 1]:
                    copy.wait()
            sem = r.out_sem[self.which]
            if self.which == FFN:
                r.s_ffn[0] = total[:, :hidden]
                r.s_ffn[1] = total[:, hidden:]
                self.hbm[t] = [
                    pltpu.make_async_copy(r.s_ffn.at[0], r.o_up.at[t], sem.at[0]),
                    pltpu.make_async_copy(r.s_ffn.at[1], r.o_down.at[t], sem.at[1]),
                ]
            else:
                for c in range(3):
                    r.s_qkv[c] = total[:, c * share : (c + 1) * share]
                r.s_out[...] = total[:, 3 * share :].T
                self.hbm[t] = [
                    pltpu.make_async_copy(r.s_qkv, r.o_qkv.at[t], sem.at[0]),
                    pltpu.make_async_copy(r.s_out, r.o_out.at[t], sem.at[1]),
                ]
            for copy in self.hbm[t]:
                copy.start()

    gx = [Gather(r.x[t]) for t in range(TOWERS)]
    gdy = [Gather(r.dy[t]) for t in range(TOWERS)]
    gp = Gather(r.pfull)
    ar1 = [AllReduce(t, FIRST) for t in range(TOWERS)]
    ar2 = [AllReduce(t, SECOND) for t in range(TOWERS)]
    rs1 = [Scatter(t, FIRST) for t in range(TOWERS)]
    rs2 = [Scatter(t, SECOND) for t in range(TOWERS)]
    stats = [Stats(t) for t in range(TOWERS)]
    grad_b, grad_c = GradSum(FFN), GradSum(ATTN)

    def attn_load(use):
        t, slot = use % TOWERS, use % 2
        pairs = ((r.wqkv, r.wqkv_v), (r.wout, r.wout_v))
        return [
            pltpu.make_async_copy(src.at[t], dst.at[slot], r.w_sem.at[6 + 2 * use + i])
            for i, (src, dst) in enumerate(pairs)
        ]

    attn_w = [attn_load(use) for use in range(2 * TOWERS)]
    ffn_w = [
        [
            pltpu.make_async_copy(r.wup.at[t], r.wup_v, r.w_sem.at[2 * t]),
            pltpu.make_async_copy(r.wdown.at[t], r.wdown_v, r.w_sem.at[2 * t + 1]),
        ]
        for t in range(TOWERS)
    ]

    def transpose_into(dst, src, rows, cols):
        for at in range(0, rows, TILE):
            size = min(TILE, rows - at)
            dst[:cols, at : at + size] = src[at : at + size, :].T

    def stage_in(ref, t, source):
        length, padded = plan.length[t], plan.padded[t]
        for e in range(plan.examples[t]):
            base = e * padded
            if length < padded:
                first = length // 128 * 128
                ref[own, base + first : base + padded] = jnp.zeros((share, padded - first), BF16)
            ref[own, base : base + length] = source[e]

    def a_norm(t):
        gain, shift = full_col(t, 0), full_col(t, 2)

        def body(ls):
            x = r.x[t][:, ls].astype(F32)
            mean = jnp.sum(x, axis=0, keepdims=True) / width
            center = x - mean
            inv = lax.rsqrt(jnp.sum(center * center, axis=0, keepdims=True) / width + EPSILON)
            r.n[t][:, ls] = (center * inv * gain + shift).astype(BF16)
            r.row[t][0:1, ls] = mean
            r.row[t][1:2, ls] = inv

        lanes_loop(plan.lanes[t], 128, body)

    def a_qkv(t):
        for copy in attn_w[t]:
            copy.wait()
        bias = jnp.concatenate(
            [own_col(t, 5), jnp.zeros((share, 1), F32), own_col(t, 6)], axis=0
        )

        def body(ls):
            value = nn(r.wqkv_v[t % 2], r.n[t][:, ls]) + bias
            r.qkv[t][:, ls] = value.astype(BF16)

        lanes_loop(plan.lanes[t], TILE, body)

    def valid_keys(t, e):
        if t == 0:
            return plan.length[0]
        if t == 1:
            return r.lengths[e]
        return r.lengths[plan.examples[1] + e] + (PATCHES + 1)

    def a_heads(t):
        padded = plan.padded[t]
        key_at = lax.broadcasted_iota(jnp.int32, (padded, 1), 0)
        qkv = r.qkv[t]
        for e in range(plan.examples[t]):
            base = e * padded
            valid = key_at < valid_keys(t, e)

            def head(h, carry):
                rows_q = block(h, HEAD_DIM)
                rows_k = block(h + heads, HEAD_DIM)
                rows_v = block(h + 2 * heads, HEAD_DIM)
                rows_m = block(h + plan.pad // HEAD_DIM, HEAD_DIM)
                keys = qkv[rows_k, base : base + padded].T
                values = qkv[rows_v, base : base + padded]
                for q in range(padded // TILE):
                    at = base + q * TILE
                    s = nn(keys, qkv[rows_q, at : at + TILE]) * (HEAD_DIM**-0.5)
                    s = jnp.where(valid, s, -1000000000.0)
                    p = jnp.exp(s - jnp.max(s, axis=0, keepdims=True))
                    p = (p * (1.0 / jnp.sum(p, axis=0, keepdims=True))).astype(BF16)
                    r.p[t][e * heads + h, :, q * TILE : (q + 1) * TILE] = p
                    r.m[t][rows_m, at : at + TILE] = nn(values, p).astype(BF16)
                return carry

            lax.fori_loop(0, heads, head, 0)

    def a_out(t):
        transpose_into(r.up_t, r.wout_v.at[t % 2], share, width)

        def body(ls):
            mixed = r.m[t][plan.pad :, ls]
            r.part[t][:, ls] = nn(r.up_t[:, :share], mixed).astype(BF16)

        lanes_loop(plan.lanes[t], TILE, body)
        ar1[t].begin()
        for copy in attn_w[t + 2]:
            copy.start()

    def b_main(t):
        for copy in ffn_w[t]:
            copy.wait()
        transpose_into(r.up_t, r.wup_v, width, hidden)
        transpose_into(r.down_t, r.wdown_v, hidden, width)
        out_bias, gain, shift = full_col(t, 4), full_col(t, 1), full_col(t, 3)
        up_bias = jnp.concatenate([own_col(t, 8 + j) for j in range(hidden // share)], axis=0)
        ar1[t].free()

        def body(ls):
            x, s = r.x[t], r.sums[FIRST][t]
            resid = x[:, ls].astype(F32) + (s[:, ls].astype(F32) + out_bias)
            r.own[t][:, ls] = x[own, ls].astype(F32) + (s[own, ls].astype(F32) + own_col(t, 4))
            mean = jnp.sum(resid, axis=0, keepdims=True) / width
            center = resid - mean
            inv = lax.rsqrt(jnp.sum(center * center, axis=0, keepdims=True) / width + EPSILON)
            xhat = center * inv
            r.row[t][2:3, ls] = inv
            normed = (xhat * gain + shift).astype(BF16)
            s[:, ls] = xhat.astype(BF16)
            r.work_n[:, ls] = normed
            h = nn(r.up_t[...], normed) + up_bias
            cdf = 0.5 * (1.0 + lax.erf(h * INV_SQRT2))
            r.work_a[:, ls] = (h * cdf).astype(BF16)
            slope = cdf + h * (jnp.exp(-0.5 * (h * h)) * INV_SQRT_2PI)
            dact = nn(r.wdown_v[...], r.dy[t][:, ls])
            dhid = (dact * slope).astype(BF16)
            r.work_h[:hidden, ls] = dhid
            r.part[t][:, ls] = nn(r.wup_v[...], dhid).astype(BF16)

        lanes_loop(plan.lanes[t], TILE, body)
        ar2[t].begin()

    def b_ffn(t):
        def body(ls):
            r.rpart[t][:, ls] = nn(r.down_t[...], r.work_a[:, ls]).astype(BF16)

        lanes_loop(plan.lanes[t], TILE, body)
        rs1[t].begin()

    def spread(dst, value, ls):
        for b in range(plan.halves * nz):
            part = value[b * plan.slab : (b + 1) * plan.slab].astype(BF16)
            dst[b % plan.halves, b // plan.halves, :, ls] = part

    def b_grad(t):
        lanes = plan.lanes[t]

        def step(at, carry):
            rows = block(at, TILE)
            value = nt(r.work_n[:, :lanes], r.work_h[rows, :lanes])
            spread(r.g_all[FFN], value, rows)
            value = nt(r.dy[t][...], r.work_a[rows, :lanes])
            spread(r.g_all[FFN], value, block(at + hidden // TILE, TILE))
            return carry

        lax.fori_loop(0, hidden // TILE, step, 0)
        grad_b.send(t)
        for j in range(hidden // share):
            keep_sum(t, 3 + j, r.work_h[j * share : (j + 1) * share, :lanes])
        keep_sum(t, 7, r.dy[t][own])

    def y_out(t):
        rs1[t].finish()
        value = r.own[t][...] + (
            r.rpart[t][own].astype(F32) + r.rfar[FIRST][t][...].astype(F32) + own_col(t, 7)
        )
        padded = plan.padded[t]
        for e in range(plan.examples[t]):
            out = value[:, e * padded : e * padded + plan.length[t]]
            r.o_y[t][e] = out.astype(BF16)

    def c_norm(t):
        ar2[t].finish()
        for copy in attn_w[TOWERS + t]:
            copy.wait()
        slot = (TOWERS + t) % 2
        gain, gain_own = full_col(t, 1), own_col(t, 1)

        def body(ls):
            dn, xhat = r.sums[SECOND][t], r.sums[FIRST][t]
            xh = xhat[:, ls].astype(F32)
            e = dn[:, ls].astype(F32) * gain
            m1 = jnp.sum(e, axis=0, keepdims=True) / width
            m2 = jnp.sum(e * xh, axis=0, keepdims=True) / width
            inv = r.row[t][2:3, ls]
            dres = r.dy[t][:, ls].astype(F32) + inv * (e - m1 - xh * m2)
            r.work_n[:, ls] = dres.astype(BF16)
            e_own = dn[own, ls].astype(F32) * gain_own
            r.own[t][:, ls] = r.dy[t][own, ls].astype(F32) + inv * (
                e_own - m1 - xhat[own, ls].astype(F32) * m2
            )

        lanes_loop(plan.lanes[t], 128, body)

        def mix(ls):
            r.work_m[:, ls] = nn(r.wout_v[slot], r.work_n[:, ls]).astype(BF16)

        lanes_loop(plan.lanes[t], TILE, mix)

    def c_heads(t):
        padded = plan.padded[t]
        qkv = r.qkv[t]
        scale = HEAD_DIM**-0.5
        for e in range(plan.examples[t]):
            base = e * padded

            def head(h, carry):
                rows_q = block(h, HEAD_DIM)
                rows_k = block(h + heads, HEAD_DIM)
                rows_v = block(h + 2 * heads, HEAD_DIM)
                keys = qkv[rows_k, base : base + padded]
                values = qkv[rows_v, base : base + padded].T
                dk = dv = None
                for q in range(padded // TILE):
                    at = base + q * TILE
                    dm = r.work_m[rows_q, at : at + TILE]
                    p = r.p[t][e * heads + h, :, q * TILE : (q + 1) * TILE]
                    dp = nn(values, dm)
                    pf = p.astype(F32)
                    delta = jnp.sum(pf * dp, axis=0, keepdims=True)
                    ds = (pf * (dp - delta)).astype(BF16)
                    dq = nn(keys, ds) * scale
                    r.work_h[rows_q, at : at + TILE] = dq.astype(BF16)
                    dk_q = nt(qkv[rows_q, at : at + TILE], ds)
                    dv_q = nt(dm, p)
                    dk = dk_q if dk is None else dk + dk_q
                    dv = dv_q if dv is None else dv + dv_q
                r.work_h[rows_k, base : base + padded] = (dk * scale).astype(BF16)
                r.work_h[rows_v, base : base + padded] = dv.astype(BF16)
                return carry

            lax.fori_loop(0, heads, head, 0)

    def c_norm_in(t):
        transpose_into(r.up_t, r.wqkv_v.at[(TOWERS + t) % 2], 3 * share, width)
        gain = full_col(t, 0)
        rs1[t].free()

        def body(ls):
            dn = nn(r.up_t[:, : 3 * share], r.work_h[: 3 * share, ls])
            e = dn * gain
            xhat = (r.x[t][:, ls].astype(F32) - r.row[t][0:1, ls]) * r.row[t][1:2, ls]
            r.stat_own[t][0:1, ls] = jnp.sum(e, axis=0, keepdims=True)
            r.stat_own[t][1:2, ls] = jnp.sum(e * xhat, axis=0, keepdims=True)
            r.rpart[t][:, ls] = dn.astype(BF16)

        lanes_loop(plan.lanes[t], TILE, body)
        rs2[t].begin()
        stats[t].begin()
        if t == 0:
            for copy in attn_w[5]:
                copy.start()

    def c_grad(t):
        lanes = plan.lanes[t]
        r.work_h[3 * share :, :lanes] = jnp.zeros((width - 3 * share, lanes), BF16)
        whole = 3 * share // TILE

        def step(at, carry):
            rows = block(at, TILE)
            spread(r.g_all[ATTN], nt(r.n[t][...], r.work_h[rows, :lanes]), rows)
            return carry

        lax.fori_loop(0, whole, step, 0)
        last = slice(whole * TILE, (whole + 1) * TILE)
        value = nt(r.n[t][...], r.work_h[last, :lanes])
        value = value + nt(r.work_n[:, :lanes], r.m[t][...])
        spread(r.g_all[ATTN], value, last)
        grad_c.send(t)
        keep_sum(t, 0, r.work_h[:share, :lanes])
        keep_sum(t, 1, r.work_h[2 * share : 3 * share, :lanes])
        keep_sum(t, 2, r.work_n[own, :lanes])
        dn, xhat = r.sums[SECOND][t], r.sums[FIRST][t]
        keep_sum(t, 9, dn[own].astype(F32) * xhat[own].astype(F32))
        keep_sum(t, 11, dn[own])

    def last_norm(t):
        rs2[t].finish()
        stats[t].finish()
        gain = own_col(t, 0)
        dn = r.rpart[t][own].astype(F32) + r.rfar[SECOND][t][...].astype(F32)
        total = r.stat_chip[t][...] + r.stat_far[t][...]
        inv = r.row[t][1:2, :]
        xhat = (r.x[t][own].astype(F32) - r.row[t][0:1, :]) * inv
        value = r.own[t][...] + inv * (
            dn * gain - total[0:1] / width - xhat * (total[1:2] / width)
        )
        padded = plan.padded[t]
        for e in range(plan.examples[t]):
            out = value[:, e * padded : e * padded + plan.length[t]]
            r.o_dx[t][e] = out.astype(BF16)
        keep_sum(t, 8, dn * xhat)
        keep_sum(t, 10, dn)

    def small_out():
        small = r.small
        if not plan.fused:
            r.o_small[...] = small[...]
            return
        copy = launch(remote(small, r.small_y, y_peer))
        copy.wait_recv()
        r.small_z[z_at] = small[...] + r.small_y[...]
        copies = []
        for k in range(1, nz):
            slot = r.small_z.at[z_at]
            copies.append(launch(remote(slot, slot, z_peer(k))))
        for copy in copies:
            copy.wait_recv()
        total = r.small_z[0]
        for k in range(1, nz):
            total = total + r.small_z[k]
        rows = total.T
        for t in range(TOWERS):
            base = t * COLS
            for j in range(2):
                r.o_qvb[t, j, :] = rows[base + j, :]
                r.o_gain[t, j, :] = rows[base + 8 + j, :]
                r.o_bias[t, j, :] = rows[base + 10 + j, :]
            r.o_outb[t, :] = rows[base + 2, :]
            r.o_downb[t, :] = rows[base + 7, :]
            for j in range(hidden // share):
                r.o_upb[t * (hidden // share) + j, :] = rows[base + 3 + j, :]

    loads = [
        pltpu.make_async_copy(src[t], dst[t], r.in_sem.at[i * TOWERS + t])
        for i, (src, dst) in enumerate(((r.in_x, r.o_y), (r.in_dy, r.o_dx)))
        for t in range(TOWERS)
    ]
    for copy in loads + attn_w[0] + attn_w[1] + ffn_w[0]:
        copy.start()
    for t in range(TOWERS):
        loads[t].wait()
        stage_in(r.x[t], t, r.o_y[t])
    r.pown[...] = r.prm[...].T
    r.pfull[own] = r.pown[...].astype(BF16)
    barrier = pltpu.get_barrier_semaphore()
    partners = [sibling, across]
    if plan.fused:
        partners += [y_peer] + [z_peer(k) for k in range(1, nz)]
    for device in partners:
        pl.semaphore_signal(barrier, inc=1, device_id=device, device_id_type=MESH)
    pl.semaphore_wait(barrier, len(partners))
    gp.start()
    gx[0].start()
    gx[1].start()
    gx[2].start()
    for t in range(TOWERS):
        loads[TOWERS + t].wait()
        stage_in(r.dy[t], t, r.o_dx[t])
        r.m[t][: plan.pad] = jnp.zeros((plan.pad, plan.lanes[t]), BF16)
        r.stat_own[t][...] = jnp.zeros_like(r.stat_own[t])
    r.small[...] = jnp.zeros_like(r.small)
    gp.forward()
    gx[0].forward()
    gp.finish()
    gx[0].finish()

    a_norm(0)
    a_qkv(0)
    gx[1].forward()
    a_heads(0)
    a_out(0)
    gx[1].finish()
    a_norm(1)
    ar1[0].cross()
    gdy[0].start()
    gx[2].forward()
    a_qkv(1)
    a_heads(1)
    a_out(1)
    gx[2].finish()
    ar1[0].back()
    a_norm(2)
    gdy[0].forward()
    ar1[1].cross()
    gdy[1].start()
    a_qkv(2)
    ar1[0].finish()
    gdy[0].finish()
    b_main(0)
    b_ffn(0)
    ar1[1].back()
    ar2[0].cross()
    rs1[0].cross()
    b_grad(0)
    for copy in ffn_w[1]:
        copy.start()
    gdy[1].forward()
    a_heads(2)
    a_out(2)
    ar2[0].back()
    grad_b.relay(0)
    ar1[1].finish()
    gdy[1].finish()
    ar1[2].cross()
    gdy[2].start()
    b_main(1)
    ar1[2].back()
    b_ffn(1)
    ar2[1].cross()
    rs1[1].cross()
    y_out(0)
    b_grad(1)
    for copy in ffn_w[2]:
        copy.start()
    gdy[2].forward()
    c_norm(0)
    c_heads(0)
    ar2[1].back()
    c_norm_in(0)
    rs2[0].cross()
    stats[0].cross()
    c_grad(0)
    grad_b.finish(0)
    grad_b.relay(1)
    ar1[2].finish()
    gdy[2].finish()
    b_main(2)
    b_ffn(2)
    ar2[2].cross()
    rs1[2].cross()
    grad_c.relay(0)
    y_out(1)
    b_grad(2)
    last_norm(0)
    c_norm(1)
    c_heads(1)
    ar2[2].back()
    c_norm_in(1)
    rs2[1].cross()
    stats[1].cross()
    c_grad(1)
    grad_b.finish(1)
    grad_b.relay(2)
    grad_c.finish(0)
    y_out(2)
    c_norm(2)
    grad_c.relay(1)
    c_heads(2)
    c_norm_in(2)
    rs2[2].cross()
    stats[2].cross()
    c_grad(2)
    last_norm(1)
    grad_b.finish(2)
    grad_c.finish(1)
    grad_c.relay(2)
    last_norm(2)
    small_out()
    grad_c.finish(2)
    for copy in list(pending):
        sent(copy)
    for grad in (grad_b, grad_c):
        for copy in grad.hbm.get(TOWERS - 1, []):
            copy.wait()


def per_device(dp, tensor, *args):
    rows, ups = args[0:3], args[15:18]
    text_lengths, pair_lengths = args[3:5]
    qkv_w, qv_b, out_w, out_b, up_w, up_b, down_w, down_b, gain, shift = args[5:15]
    plan = Plan(rows, (qkv_w, out_w, up_w), dp, tensor)
    width, share, hidden = plan.width, plan.share, plan.hidden
    ratio = hidden // share
    nz = plan.nz

    turned = [jnp.transpose(x, (0, 2, 1)) for x in rows]
    turned_up = [jnp.transpose(x, (0, 2, 1)) for x in ups]
    wqkv = jnp.transpose(qkv_w, (0, 2, 3, 1)).reshape(TOWERS, 3 * share, width)
    columns = jnp.concatenate(
        [gain, shift, out_b[:, None], qv_b, down_b[:, None], up_b.reshape(TOWERS, ratio, share)],
        axis=1,
    ).reshape(TOWERS * COLS, share)
    columns = jnp.pad(columns, ((0, 128 - TOWERS * COLS), (0, 0))).astype(F32)
    lengths = jnp.concatenate([text_lengths, pair_lengths])

    vmem = pl.BlockSpec(memory_space=pltpu.VMEM)
    hbm = pl.BlockSpec(memory_space=pl.ANY)
    smem = pl.BlockSpec(memory_space=pltpu.SMEM)

    ins, specs = SimpleNamespace(), SimpleNamespace()
    ins.in_x, specs.in_x = turned, [hbm] * TOWERS
    ins.in_dy, specs.in_dy = turned_up, [hbm] * TOWERS
    ins.prm, specs.prm = columns, vmem
    ins.lengths, specs.lengths = lengths, smem
    ins.wqkv, specs.wqkv = wqkv, hbm
    ins.wout, specs.wout = out_w, hbm
    ins.wup, specs.wup = up_w, hbm
    ins.wdown, specs.wdown = down_w, hbm

    outs = SimpleNamespace()
    outs.o_y = [Out(vmem, x.shape, BF16) for x in turned]
    outs.o_dx = [Out(vmem, x.shape, BF16) for x in turned]
    if plan.fused:
        outs.o_qkv = Out(hbm, (TOWERS, 3, plan.slab, share))
        outs.o_out = Out(hbm, (TOWERS, share, plan.slab))
        outs.o_up = Out(hbm, (TOWERS, plan.slab, hidden))
        outs.o_down = Out(hbm, (TOWERS, plan.slab, hidden))
        outs.o_qvb = Out(vmem, (TOWERS, 2, share))
        outs.o_outb = Out(vmem, (TOWERS, share))
        outs.o_upb = Out(vmem, (TOWERS * ratio, share))
        outs.o_downb = Out(vmem, (TOWERS, share))
        outs.o_gain = Out(vmem, (TOWERS, 2, share))
        outs.o_bias = Out(vmem, (TOWERS, 2, share))
    else:
        outs.o_g = [Out(hbm, (TOWERS, width, n), BF16) for n in plan.grad_lanes]
        outs.o_small = Out(vmem, (share, 128))

    room = scratch(plan)
    in_refs, in_tree = flatten(vars(ins))
    out_refs, out_tree = flatten(vars(outs))
    room_refs, room_tree = flatten(vars(room))

    def body(*refs):
        first, second = len(in_refs), len(in_refs) + len(out_refs)
        r = SimpleNamespace()
        vars(r).update(jax.tree.unflatten(in_tree, refs[:first]))
        vars(r).update(jax.tree.unflatten(out_tree, refs[first:second]))
        vars(r).update(jax.tree.unflatten(room_tree, refs[second:]))
        kernel(plan, r)

    results = pl.pallas_call(
        body,
        out_shape=[jax.ShapeDtypeStruct(out.shape, out.dtype) for out in out_refs],
        in_specs=flatten(vars(specs))[0],
        out_specs=[out.spec for out in out_refs],
        scratch_shapes=room_refs,
        compiler_params=pltpu.CompilerParams(
            collective_id=1, has_side_effects=True, vmem_limit_bytes=67043328
        ),
        name="layer",
    )(*in_refs)
    got = SimpleNamespace(**jax.tree.unflatten(out_tree, results))

    if not plan.fused:
        sums_b, sums_c = [
            lax.psum_scatter(g.astype(F32), "dp", scatter_dimension=1, tiled=True)
            for g in got.o_g
        ]
        small = lax.psum(got.o_small, "dp").T[: TOWERS * COLS].reshape(TOWERS, COLS, share)
        got.o_up, got.o_down = sums_b[:, :, :hidden], sums_b[:, :, hidden:]
        slab = sums_c.shape[1]
        qkv = sums_c[:, :, : 3 * share].reshape(TOWERS, slab, 3, share)
        got.o_qkv = jnp.transpose(qkv, (0, 2, 1, 3))
        got.o_out = jnp.transpose(sums_c[:, :, 3 * share :], (0, 2, 1))
        got.o_qvb, got.o_outb = small[:, 0:2], small[:, 2]
        got.o_upb, got.o_downb = small[:, 3 : 3 + ratio], small[:, 7]
        got.o_gain, got.o_bias = small[:, 8:10], small[:, 10:12]

    return (
        *[jnp.transpose(y, (0, 2, 1)) for y in got.o_y],
        *[jnp.transpose(dx, (0, 2, 1)) for dx in got.o_dx],
        jnp.transpose(got.o_qkv, (0, 2, 1, 3)),
        got.o_qvb,
        got.o_out,
        got.o_outb,
        got.o_up,
        got.o_upb.reshape(TOWERS, hidden),
        jnp.transpose(got.o_down, (0, 2, 1)),
        got.o_downb,
        got.o_gain,
        got.o_bias,
    )


def solution(mesh):
    dp, tensor = mesh.shape["dp"], mesh.shape["tensor"]

    def step(*args):
        return per_device(dp, tensor, *args)

    rows = P("dp", None, "tensor")
    return jax.shard_map(
        step,
        mesh=mesh,
        in_specs=(
            rows,
            rows,
            rows,
            P("dp"),
            P("dp"),
            P(None, None, None, "tensor"),
            P(None, None, "tensor"),
            P(None, "tensor", None),
            P(None, "tensor"),
            P(None, None, "tensor"),
            P(None, "tensor"),
            P(None, "tensor", None),
            P(None, "tensor"),
            P(None, None, "tensor"),
            P(None, None, "tensor"),
            rows,
            rows,
            rows,
        ),
        out_specs=(
            rows,
            rows,
            rows,
            rows,
            rows,
            rows,
            P(None, "dp", None, "tensor"),
            P(None, None, "tensor"),
            P(None, "tensor", "dp"),
            P(None, "tensor"),
            P(None, "dp", "tensor"),
            P(None, "tensor"),
            P(None, "tensor", "dp"),
            P(None, "tensor"),
            P(None, None, "tensor"),
            P(None, None, "tensor"),
        ),
        check_vma=False,
    )
```

time: 1030 us -> 250 us (0.24); the launches traced: 1010 us -> 249 us
  waiting for transfers between devices: 415 us -> 0 us
  Pallas kernels: 0 us -> 224 us
  local copies, waits for them, and re-layouts: 204 us -> 22 us
  blocking collectives: 171 us -> 0 us
  matrix products: 106 us -> 0 us
  other arithmetic: 96.2 us -> 1.25 us
  between operations: 19.6 us -> 2 us
    unnamed x26 -> x0, waiting for transfers between devices: 233 us -> none
    pallas_call x0 -> x1, Pallas kernels: none -> 224 us  [per_device(): pl.pallas_call(body, out_shape=[jax.ShapeDtypeStruct(out.shape, out.dtype...]
    unnamed x514 -> x31, local copies, waits for them, and re-layouts: 160 us -> 17.5 us
    reduce_scatter x1 -> x0, waiting for transfers between devices: 130 us -> none  [per_device(): lax.psum_scatter(stacked[2], 'dp', scatter_dimension=1, tiled=True)]
    all_gather x12 -> x0, blocking collectives: 101 us -> none  [the longest x4 38.1 us: gather_grads(): return lax.all_gather(value, 'tensor', axis=2, tiled=True)]
    dot_general x50 -> x0, matrix products: 101 us -> none  [the longest x3 18 us: forward_tower(): jnp.einsum('eld,df->elf', normed_two, up_w, preferred_element_type=jnp.fl...]
    psum x3 -> x0, blocking collectives: 61 us -> none  [the longest x1 38.3 us: per_device(): small_grads = lax.psum(stacked[4], 'dp')]
    psum x2 -> x0, waiting for transfers between devices: 51.7 us -> none  [forward_tower(): lax.psum(rounded(partial_value).astype(jnp.bfloat16), 'tensor')]
  transfers between devices with their start and end apart: 16 -> 0, of which waited for: 4 -> 0; matrix products, arithmetic and copies ran while one was open for 34% -> 0% of each run, Pallas kernels for 0% -> 0%
where the time goes in v1:
time: 250 us; the launch traced here: 249 us
  Pallas kernels  224 us (90%)
  local copies, waits for them, and re-layouts  22 us (9%)
    pallas_call x1, Pallas kernels, per_device(): pl.pallas_call(body, out_shape=[jax.ShapeDtypeStruct(out.shape, out.dtype...  224 us
    unnamed x31, local copies, waits for them, and re-layouts  17.5 us

profile of v1, /device:TPU:0, one launch (start us, length us, event | category | flops | bytes accessed | tf_op | source)
XLA Modules:
  0.0 249.3 jit_solution(1383830267164886743)
XLA Ops:
  1.9 0.6 pad_add_fusion.refs_6_
  2.5 0.7 copy.34
  3.2 0.7 copy.35
  3.9 0.8 reshape.44
  4.7 0.8 concatenate.7
  5.5 0.7 pad_convert_fusion.refs_7_
  6.1 224.0 %layer.1 = (f32[3,2,192]{2,1,0:T(2,128)}, f32[3,96,768]{2,1,0:T(8,128)}, f32[3,192]{1,0:T(4,128)}, bf16[2,192,197]{2,1,0:T(8,128)(2,1)}, bf16[1,192,512]{2,1,0:T...) custom-call(bf16[2,192,197]{2,1,0:T(8,128)(2,1)} %bitcast.30, ...), custom_call_target="tpu_custom_call" | custom-call | tf_op jit(solution)/shard_map/layer/pallas_call | solution.py:897
  230.1 0.0 copy-start.5
  230.1 0.0 copy-start.2
  230.2 0.0 copy-start.7
  230.2 0.0 copy-start.1
  230.2 0.0 copy-start
  230.2 1.5 reshape.47
  231.7 1.6 copy.53
  233.3 1.6 copy.54
  235.0 1.7 copy.55
  236.7 1.6 copy.56
  238.3 0.0 copy-start.6
  238.3 0.0 copy-start.4
  238.3 0.0 copy-start.3
  238.3 1.6 copy.57
  239.9 1.7 copy.58
  241.6 2.1 copy.59
  243.7 0.0 copy-done.5
  243.7 0.6 copy.60
  244.3 0.0 copy-done.2
  244.3 0.7 copy.61
  245.1 0.0 copy-done.7
  245.1 0.6 copy.62
  245.7 0.0 copy-done.1
  245.7 0.9 copy.63
  246.6 0.0 copy-done
  246.6 0.9 copy.64
  247.5 0.0 copy-done.6
  247.5 0.6 copy.65
  248.1 0.0 copy-done.4
  248.1 0.6 copy.66
  248.7 0.0 copy-done.3
  248.7 0.6 copy.67
  (1 shorter events, 0.0 us)
Async XLA Ops:
  230.1 13.6 %copy-start.5 = (f32[3,2,192]{2,1,0:T(2,128)S(1)}, f32[3,2,192]{2,1,0:T(2,128)}, u32[]{:S(2)}) copy-start(f32[3,2,192]{2,1,0:T(2,128)} %get-tuple-element.71) | copy-start | bytes 13828
  230.1 14.2 %copy-start.2 = (f32[3,192,96]{2,1,0:T(8,128)S(1)}, f32[3,192,96]{2,1,0:T(8,128)}, u32[]{:S(2)}) copy-start(f32[3,192,96]{2,1,0:T(8,128)} %get-tuple-element.72) | copy-start | bytes 663556
  230.2 14.9 %copy-start.7 = (f32[3,192]{1,0:T(4,128)S(1)}, f32[3,192]{1,0:T(4,128)}, u32[]{:S(2)}) copy-start(f32[3,192]{1,0:T(4,128)} %get-tuple-element.73) | copy-start | bytes 6916
  230.2 15.5 %copy-start.1 = (f32[3,96,768]{2,1,0:T(8,128)S(1)}, f32[3,96,768]{2,1,0:T(8,128)}, u32[]{:S(2)}) copy-start(f32[3,96,768]{2,1,0:T(8,128)} %get-tuple-element.74) | copy-start | bytes 2654212
  230.2 16.4 %copy-start = (f32[3,96,768]{2,1,0:T(8,128)S(1)}, f32[3,96,768]{2,1,0:T(8,128)}, u32[]{:S(2)}) copy-start(f32[3,96,768]{2,1,0:T(8,128)} %get-tuple-element.44) | copy-start | bytes 2654212
  238.3 9.2 %copy-start.6 = (f32[3,192]{1,0:T(4,128)S(1)}, f32[3,192]{1,0:T(4,128)}, u32[]{:S(2)}) copy-start(f32[3,192]{1,0:T(4,128)} %get-tuple-element.77) | copy-start | bytes 6916
  238.3 9.8 %copy-start.4 = (f32[3,2,192]{2,1,0:T(2,128)S(1)}, f32[3,2,192]{2,1,0:T(2,128)}, u32[]{:S(2)}) copy-start(f32[3,2,192]{2,1,0:T(2,128)} %get-tuple-element.78) | copy-start | bytes 13828
  238.3 10.4 %copy-start.3 = (f32[3,2,192]{2,1,0:T(2,128)S(1)}, f32[3,2,192]{2,1,0:T(2,128)}, u32[]{:S(2)}) copy-start(f32[3,2,192]{2,1,0:T(2,128)} %get-tuple-element.79) | copy-start | bytes 13828

commit v2 on v1

--- a/solution.py
+++ b/solution.py
@@ -12,10 +12,25 @@
 EPSILON = 1e-06
 TOWERS = 3
 FIRST, SECOND = 0, 1
-FFN, ATTN = 0, 1
+UP, DOWN, ATTN = 0, 1, 2
+RING = 3
+UNITS = (
+    (0, DOWN),
+    (0, UP),
+    (1, DOWN),
+    (1, UP),
+    (0, ATTN),
+    (2, DOWN),
+    (2, UP),
+    (1, ATTN),
+    (2, ATTN),
+)
 TILE = 256
 COLS = 12
 N_REMOTE = 160
+EARLY, LATE = 32, 8
+SMALL = EARLY + LATE
+LATE_COLS = (0, 1, 2, 8, 9, 10, 11)
 BF16 = jnp.bfloat16
 F32 = jnp.float32
 MESH = pl.DeviceIdType.MESH
@@ -47,14 +62,21 @@
         self.share = out.shape[1]
         self.hidden = upw.shape[2]
         self.heads = self.share // HEAD_DIM
-        self.grad_lanes = (2 * self.hidden, 4 * self.share)
         self.pad = (3 * self.share) % TILE
         assert tensor == 4 and self.width == 4 * self.share
-        assert self.pad + self.share == TILE and self.hidden % TILE == 0
+        assert self.pad + self.share == TILE and self.hidden == self.width
         self.fused = dp % 2 == 0 and dp > 1 and self.width % (16 * dp) == 0
         self.nz = dp // 2 if self.fused else 1
         self.slab = self.width // dp if self.fused else self.width
         self.halves = 2 if self.fused else 1
+
+
+def small_row(t, j):
+    if t < TOWERS - 1:
+        return t * COLS + j
+    if j in LATE_COLS:
+        return EARLY + LATE_COLS.index(j)
+    return t * COLS + [c for c in range(COLS) if c not in LATE_COLS].index(j)
 
 
 class Out:
@@ -88,28 +110,27 @@
     k.own, k.row = each(share, dtype=F32), each(8, dtype=F32)
     k.stat_own, k.stat_near = each(8, dtype=F32), each(8, dtype=F32)
     k.stat_chip, k.stat_far = each(8, dtype=F32), each(8, dtype=F32)
-    land = plan.slab if plan.fused else 16
-    k.g_all = [vm(plan.halves, nz, plan.slab, n) for n in plan.grad_lanes]
-    k.g_y = [vm(nz, land, n) for n in plan.grad_lanes]
-    k.g_z = [vm(nz, land, n) for n in plan.grad_lanes]
-    k.credit = [pltpu.SemaphoreType.REGULAR for _ in plan.grad_lanes]
-    k.out_sem = [dma((2,)) for _ in plan.grad_lanes]
+    k.g_all = vm(RING, plan.halves, nz, plan.slab, width)
+    k.credit = pltpu.SemaphoreType.REGULAR((RING,))
+    k.out_sem = dma((4,))
     if plan.fused:
-        k.g_far = [
-            [vm(max(nz - 1, 1), plan.slab, n) for _ in range(TOWERS)] for n in plan.grad_lanes
-        ]
+        k.g_y = vm(RING, nz, plan.slab, width)
+        k.g_z = vm(RING, nz, plan.slab, width)
+        k.g_far = vm(len(UNITS), max(nz - 1, 1), plan.slab, width)
         k.s_ffn = vm(2, plan.slab, hidden, dtype=F32)
         k.s_qkv = vm(3, plan.slab, share, dtype=F32)
         k.s_out = vm(share, plan.slab, dtype=F32)
+        k.rows = [vm(n, share, dtype=F32) for n in (EARLY, LATE)]
+        k.rows_y = [vm(n, share, dtype=F32) for n in (EARLY, LATE)]
+        k.rows_z = [vm(nz, n, share, dtype=F32) for n in (EARLY, LATE)]
     k.wqkv_v, k.wout_v = vm(2, 3 * share, width), vm(2, share, width)
     k.wup_v, k.wdown_v = vm(width, hidden), vm(hidden, width)
     k.up_t, k.down_t = vm(hidden, width), vm(width, hidden)
     k.work_n, k.work_a = vm(width, most), vm(hidden, most)
     k.work_h, k.work_m = vm(width, most), vm(share, most)
     k.pown, k.pfull = vm(share, 128, dtype=F32), vm(width, 128)
-    k.small, k.small_y = vm(share, 128, dtype=F32), vm(share, 128, dtype=F32)
-    k.small_z = vm(nz, share, 128, dtype=F32)
-    k.in_sem, k.w_sem, k.part_sem = dma((2 * TOWERS,)), dma((18,)), dma((TOWERS,))
+    k.prm, k.small = vm(128, share, dtype=F32), vm(share, 128, dtype=F32)
+    k.in_sem, k.w_sem, k.part_sem = dma((2 * TOWERS,)), dma((18,)), dma(())
     k.send_sem, k.recv_sem = dma((N_REMOTE,)), dma((N_REMOTE,))
     return k
 
@@ -178,7 +199,7 @@
     def keep_sum(t, j, value):
         column = jnp.sum(value.astype(F32), axis=1, keepdims=True)
         small = r.small
-        small[...] = jnp.where(lane_of_small == t * COLS + j, column, small[...])
+        small[...] = jnp.where(lane_of_small == small_row(t, j), column, small[...])
 
     def own_col(t, j):
         return r.pown[:, t * COLS + j : t * COLS + j + 1]
@@ -285,77 +306,77 @@
         def finish(self):
             self.c2.wait_recv()
 
-    class GradSum:
-        def __init__(self, which):
-            self.all, self.land, self.sums = r.g_all[which], r.g_y[which], r.g_z[which]
-            self.credit = r.credit[which]
-            self.which = which
-            self.y_copies, self.z_copies, self.hbm = {}, {}, {}
-
-        def send(self, t):
+    class Unit:
+        def __init__(self, at, t, kind):
+            self.at, self.t, self.kind = at, t, kind
+            self.slot = at % RING
+            self.all = r.g_all.at[self.slot]
+            self.y_copies, self.z_copies, self.hbm = [], [], []
+
+        def send(self):
             if not plan.fused:
-                copy = pltpu.make_async_copy(
-                    self.all.at[0, 0], r.o_g[self.which].at[t], r.part_sem.at[t]
-                )
+                dst = r.o_g.at[self.kind, self.t]
+                copy = pltpu.make_async_copy(self.all.at[0, 0], dst, r.part_sem)
                 copy.start()
                 copy.wait()
                 return
-            if t:
-                pl.semaphore_wait(self.credit, 1)
-            self.y_copies[t] = []
+            if self.at >= RING:
+                pl.semaphore_wait(r.credit.at[self.slot], 1)
             for j in range(nz):
                 at = z_index(1 + j)
-                copy = remote(self.all.at[1 - y_at, at], self.land.at[at], y_peer)
-                self.y_copies[t].append(launch(copy))
-
-        def relay(self, t):
+                src, dst = self.all.at[1 - y_at, at], r.g_y.at[self.slot, at]
+                self.y_copies.append(launch(remote(src, dst, y_peer)))
+
+        def relay(self, quarter):
+            if plan.fused:
+                for j in range(nz * quarter // 4, nz * (quarter + 1) // 4):
+                    self.relay_piece(j)
+
+        def relay_piece(self, j):
+            if j == 0 and self.at >= RING:
+                for copy in units[self.at - RING].z_copies:
+                    sent(copy)
+            at = z_index(1 + j)
+            sums = r.g_z.at[self.slot, at]
+            self.y_copies[j].wait_recv()
+            total = self.all[y_at, at].astype(F32) + r.g_y[self.slot, at].astype(F32)
+            sums[...] = total.astype(BF16)
+            if j < nz - 1:
+                dst = r.g_far.at[self.at, j]
+                self.z_copies.append(launch(remote(sums, dst, z_peer(1 + j))))
+                return
+            for copy in self.y_copies:
+                sent(copy)
+            if self.at + RING < len(units):
+                credit = r.credit.at[self.slot]
+                pl.semaphore_signal(credit, inc=1, device_id=y_peer, device_id_type=MESH)
+
+        def finish(self):
             if not plan.fused:
                 return
-            if t:
-                for copy in self.z_copies[t - 1]:
-                    sent(copy)
-            self.z_copies[t] = []
-            for j in range(nz):
-                at = z_index(1 + j)
-                copy = self.y_copies[t][j]
-                copy.wait_recv()
-                total = self.all[y_at, at].astype(F32) + self.land[at].astype(F32)
-                self.sums[at] = total.astype(BF16)
-                if j < nz - 1:
-                    dst = r.g_far[self.which][t].at[j]
-                    self.z_copies[t].append(launch(remote(self.sums.at[at], dst, z_peer(1 + j))))
-            for copy in self.y_copies[t]:
-                sent(copy)
-            if t < TOWERS - 1:
-                pl.semaphore_signal(self.credit, inc=1, device_id=y_peer, device_id_type=MESH)
-
-        def finish(self, t):
-            if not plan.fused:
-                return
-            total = self.sums[z_at].astype(F32)
+            total = r.g_z[self.slot, z_at].astype(F32)
             for j in range(nz - 1):
-                self.z_copies[t][j].wait_recv()
-                total = total + r.g_far[self.which][t][j].astype(F32)
-            if t:
-                for copy in self.hbm[t - 1]:
-                    copy.wait()
-            sem = r.out_sem[self.which]
-            if self.which == FFN:
-                r.s_ffn[0] = total[:, :hidden]
-                r.s_ffn[1] = total[:, hidden:]
-                self.hbm[t] = [
-                    pltpu.make_async_copy(r.s_ffn.at[0], r.o_up.at[t], sem.at[0]),
-                    pltpu.make_async_copy(r.s_ffn.at[1], r.o_down.at[t], sem.at[1]),
-                ]
+                self.z_copies[j].wait_recv()
+                total = total + r.g_far[self.at, j].astype(F32)
+            t, sem = self.t, r.out_sem
+            for before in units[: self.at]:
+                if before.kind == self.kind:
+                    for copy in before.hbm:
+                        copy.wait()
+                    before.hbm = []
+            if self.kind == UP or self.kind == DOWN:
+                out = r.o_up if self.kind == UP else r.o_down
+                r.s_ffn[self.kind] = total
+                self.hbm = [pltpu.make_async_copy(r.s_ffn.at[self.kind], out.at[t], sem.at[self.kind])]
             else:
                 for c in range(3):
                     r.s_qkv[c] = total[:, c * share : (c + 1) * share]
                 r.s_out[...] = total[:, 3 * share :].T
-                self.hbm[t] = [
-                    pltpu.make_async_copy(r.s_qkv, r.o_qkv.at[t], sem.at[0]),
-                    pltpu.make_async_copy(r.s_out, r.o_out.at[t], sem.at[1]),
+                self.hbm = [
+                    pltpu.make_async_copy(r.s_qkv, r.o_qkv.at[t], sem.at[2]),
+                    pltpu.make_async_copy(r.s_out, r.o_out.at[t], sem.at[3]),
                 ]
-            for copy in self.hbm[t]:
+            for copy in self.hbm:
                 copy.start()
 
     gx = [Gather(r.x[t]) for t in range(TOWERS)]
@@ -366,7 +387,10 @@
     rs1 = [Scatter(t, FIRST) for t in range(TOWERS)]
     rs2 = [Scatter(t, SECOND) for t in range(TOWERS)]
     stats = [Stats(t) for t in range(TOWERS)]
-    grad_b, grad_c = GradSum(FFN), GradSum(ATTN)
+    units = []
+    for at, (t, kind) in enumerate(UNITS):
+        units.append(Unit(at, t, kind))
+    unit_of = {(unit.t, unit.kind): unit for unit in units}
 
     def attn_load(use):
         t, slot = use % TOWERS, use % 2
@@ -399,6 +423,23 @@
                 ref[own, base + first : base + padded] = jnp.zeros((share, padded - first), BF16)
             ref[own, base : base + length] = source[e]
 
+    def param_rows():
+        prm = r.prm
+        prm[...] = jnp.zeros_like(prm)
+        up_bias = r.in_up_b[...].astype(F32)
+        for t in range(TOWERS):
+            base = t * COLS
+            for j in range(2):
+                prm[base + j, :] = r.in_gain[t, j, :].astype(F32)
+                prm[base + 2 + j, :] = r.in_shift[t, j, :].astype(F32)
+                prm[base + 5 + j, :] = r.in_qv_b[t, j, :].astype(F32)
+            prm[base + 4, :] = r.in_out_b[t, :].astype(F32)
+            prm[base + 7, :] = r.in_down_b[t, :].astype(F32)
+            for j in range(hidden // share):
+                prm[base + 8 + j, :] = up_bias[t, j * share : (j + 1) * share]
+        r.pown[...] = prm[...].T
+        r.pfull[own] = r.pown[...].astype(BF16)
+
     def a_norm(t):
         gain, shift = full_col(t, 0), full_col(t, 2)
 
@@ -430,13 +471,14 @@
         if t == 0:
             return plan.length[0]
         if t == 1:
-            return r.lengths[e]
-        return r.lengths[plan.examples[1] + e] + (PATCHES + 1)
+            return r.in_text[e]
+        return r.in_pair[e] + (PATCHES + 1)
 
     def a_heads(t):
         padded = plan.padded[t]
         key_at = lax.broadcasted_iota(jnp.int32, (padded, 1), 0)
         qkv = r.qkv[t]
+        r.m[t][: plan.pad] = jnp.zeros((plan.pad, plan.lanes[t]), BF16)
         for e in range(plan.examples[t]):
             base = e * padded
             valid = key_at < valid_keys(t, e)
@@ -461,22 +503,24 @@
             lax.fori_loop(0, heads, head, 0)
 
     def a_out(t):
-        transpose_into(r.up_t, r.wout_v.at[t % 2], share, width)
+        transpose_into(r.work_a, r.wout_v.at[t % 2], share, width)
 
         def body(ls):
             mixed = r.m[t][plan.pad :, ls]
-            r.part[t][:, ls] = nn(r.up_t[:, :share], mixed).astype(BF16)
+            r.part[t][:, ls] = nn(r.work_a[:, :share], mixed).astype(BF16)
 
         lanes_loop(plan.lanes[t], TILE, body)
         ar1[t].begin()
         for copy in attn_w[t + 2]:
             copy.start()
 
-    def b_main(t):
+    def b_prep(t):
         for copy in ffn_w[t]:
             copy.wait()
         transpose_into(r.up_t, r.wup_v, width, hidden)
         transpose_into(r.down_t, r.wdown_v, hidden, width)
+
+    def b_main(t):
         out_bias, gain, shift = full_col(t, 4), full_col(t, 1), full_col(t, 3)
         up_bias = jnp.concatenate([own_col(t, 8 + j) for j in range(hidden // share)], axis=0)
         ar1[t].free()
@@ -504,6 +548,9 @@
 
         lanes_loop(plan.lanes[t], TILE, body)
         ar2[t].begin()
+        if t + 1 < TOWERS:
+            for copy in ffn_w[t + 1]:
+                copy.start()
 
     def b_ffn(t):
         def body(ls):
@@ -517,19 +564,29 @@
             part = value[b * plan.slab : (b + 1) * plan.slab].astype(BF16)
             dst[b % plan.halves, b // plan.halves, :, ls] = part
 
-    def b_grad(t):
-        lanes = plan.lanes[t]
+    def grad_loop(unit, lhs, rhs):
+        dst = unit.all
 
         def step(at, carry):
             rows = block(at, TILE)
-            value = nt(r.work_n[:, :lanes], r.work_h[rows, :lanes])
-            spread(r.g_all[FFN], value, rows)
-            value = nt(r.dy[t][...], r.work_a[rows, :lanes])
-            spread(r.g_all[FFN], value, block(at + hidden // TILE, TILE))
+            spread(dst, nt(lhs(), rhs(rows)), rows)
             return carry
 
         lax.fori_loop(0, hidden // TILE, step, 0)
-        grad_b.send(t)
+        unit.send()
+
+    def b_up(t):
+        lanes = plan.lanes[t]
+        grad_loop(
+            unit_of[t, UP], lambda: r.work_n[:, :lanes], lambda rows: r.work_h[rows, :lanes]
+        )
+
+    def b_down(t):
+        lanes = plan.lanes[t]
+        grad_loop(unit_of[t, DOWN], lambda: r.dy[t][...], lambda rows: r.work_a[rows, :lanes])
+
+    def b_sum(t):
+        lanes = plan.lanes[t]
         for j in range(hidden // share):
             keep_sum(t, 3 + j, r.work_h[j * share : (j + 1) * share, :lanes])
         keep_sum(t, 7, r.dy[t][own])
@@ -545,7 +602,6 @@
             r.o_y[t][e] = out.astype(BF16)
 
     def c_norm(t):
-        ar2[t].finish()
         for copy in attn_w[TOWERS + t]:
             copy.wait()
         slot = (TOWERS + t) % 2
@@ -606,10 +662,13 @@
 
             lax.fori_loop(0, heads, head, 0)
 
-    def c_norm_in(t):
+    def c_prep(t):
         transpose_into(r.up_t, r.wqkv_v.at[(TOWERS + t) % 2], 3 * share, width)
+
+    def c_dn(t):
         gain = full_col(t, 0)
         rs1[t].free()
+        r.stat_own[t][...] = jnp.zeros_like(r.stat_own[t])
 
         def body(ls):
             dn = nn(r.up_t[:, : 3 * share], r.work_h[: 3 * share, ls])
@@ -628,20 +687,24 @@
 
     def c_grad(t):
         lanes = plan.lanes[t]
+        unit = unit_of[t, ATTN]
         r.work_h[3 * share :, :lanes] = jnp.zeros((width - 3 * share, lanes), BF16)
         whole = 3 * share // TILE
 
         def step(at, carry):
             rows = block(at, TILE)
-            spread(r.g_all[ATTN], nt(r.n[t][...], r.work_h[rows, :lanes]), rows)
+            spread(unit.all, nt(r.n[t][...], r.work_h[rows, :lanes]), rows)
             return carry
 
         lax.fori_loop(0, whole, step, 0)
         last = slice(whole * TILE, (whole + 1) * TILE)
         value = nt(r.n[t][...], r.work_h[last, :lanes])
         value = value + nt(r.work_n[:, :lanes], r.m[t][...])
-        spread(r.g_all[ATTN], value, last)
-        grad_c.send(t)
+        spread(unit.all, value, last)
+        unit.send()
+
+    def c_sum(t):
+        lanes = plan.lanes[t]
         keep_sum(t, 0, r.work_h[:share, :lanes])
         keep_sum(t, 1, r.work_h[2 * share : 3 * share, :lanes])
         keep_sum(t, 2, r.work_n[own, :lanes])
@@ -667,167 +730,250 @@
         keep_sum(t, 8, dn * xhat)
         keep_sum(t, 10, dn)
 
-    def small_out():
-        small = r.small
+    def small_send(late):
+        rows = r.small[...].T
+        first, last = (EARLY, EARLY + LATE) if late else (0, EARLY)
+        part = rows[first:last]
         if not plan.fused:
-            r.o_small[...] = small[...]
+            r.o_rows[first:last] = part
             return
-        copy = launch(remote(small, r.small_y, y_peer))
-        copy.wait_recv()
-        r.small_z[z_at] = small[...] + r.small_y[...]
-        copies = []
+        r.rows[late][...] = part
+        small_y[late] = launch(remote(r.rows[late], r.rows_y[late], y_peer))
+
+    def small_relay(late):
+        if not plan.fused:
+            return
+        small_y[late].wait_recv()
+        r.rows_z[late][z_at] = r.rows[late][...] + r.rows_y[late][...]
         for k in range(1, nz):
-            slot = r.small_z.at[z_at]
-            copies.append(launch(remote(slot, slot, z_peer(k))))
-        for copy in copies:
+            slot = r.rows_z[late].at[z_at]
+            small_z[late].append(launch(remote(slot, slot, z_peer(k))))
+
+    def small_finish(late):
+        if not plan.fused:
+            return
+        for copy in small_z[late]:
             copy.wait_recv()
-        total = r.small_z[0]
+        total = r.rows_z[late][0]
         for k in range(1, nz):
-            total = total + r.small_z[k]
-        rows = total.T
-        for t in range(TOWERS):
-            base = t * COLS
-            for j in range(2):
-                r.o_qvb[t, j, :] = rows[base + j, :]
-                r.o_gain[t, j, :] = rows[base + 8 + j, :]
-                r.o_bias[t, j, :] = rows[base + 10 + j, :]
-            r.o_outb[t, :] = rows[base + 2, :]
-            r.o_downb[t, :] = rows[base + 7, :]
-            for j in range(hidden // share):
-                r.o_upb[t * (hidden // share) + j, :] = rows[base + 3 + j, :]
-
-    loads = [
-        pltpu.make_async_copy(src[t], dst[t], r.in_sem.at[i * TOWERS + t])
-        for i, (src, dst) in enumerate(((r.in_x, r.o_y), (r.in_dy, r.o_dx)))
-        for t in range(TOWERS)
-    ]
-    for copy in loads + attn_w[0] + attn_w[1] + ffn_w[0]:
-        copy.start()
-    for t in range(TOWERS):
-        loads[t].wait()
-        stage_in(r.x[t], t, r.o_y[t])
-    r.pown[...] = r.prm[...].T
-    r.pfull[own] = r.pown[...].astype(BF16)
+            total = total + r.rows_z[late][k]
+        if late:
+            r.o_rows[EARLY : EARLY + LATE] = total
+        else:
+            r.o_rows[:EARLY] = total
+
+    small_y, small_z = [None, None], [[], []]
+
     barrier = pltpu.get_barrier_semaphore()
     partners = [sibling, across]
     if plan.fused:
         partners += [y_peer] + [z_peer(k) for k in range(1, nz)]
     for device in partners:
         pl.semaphore_signal(barrier, inc=1, device_id=device, device_id_type=MESH)
+    loads = [
+        pltpu.make_async_copy(src[t], dst[t], r.in_sem.at[i * TOWERS + t])
+        for i, (src, dst) in enumerate(((r.in_x, r.o_y), (r.in_dy, r.o_dx)))
+        for t in range(TOWERS)
+    ]
+    for copy in loads + attn_w[0] + ffn_w[0] + attn_w[1]:
+        copy.start()
+    param_rows()
+    loads[0].wait()
+    stage_in(r.x[0], 0, r.o_y[0])
     pl.semaphore_wait(barrier, len(partners))
     gp.start()
     gx[0].start()
-    gx[1].start()
-    gx[2].start()
+    for t in range(1, TOWERS):
+        loads[t].wait()
+        stage_in(r.x[t], t, r.o_y[t])
     for t in range(TOWERS):
         loads[TOWERS + t].wait()
         stage_in(r.dy[t], t, r.o_dx[t])
-        r.m[t][: plan.pad] = jnp.zeros((plan.pad, plan.lanes[t]), BF16)
-        r.stat_own[t][...] = jnp.zeros_like(r.stat_own[t])
     r.small[...] = jnp.zeros_like(r.small)
     gp.forward()
+    gx[1].start()
+    gp.finish()
+    gdy[0].start()
+    b_prep(0)
     gx[0].forward()
-    gp.finish()
     gx[0].finish()
-
     a_norm(0)
     a_qkv(0)
-    gx[1].forward()
     a_heads(0)
     a_out(0)
+    ar1[0].cross()
+    gdy[0].forward()
+    gx[1].forward()
     gx[1].finish()
     a_norm(1)
-    ar1[0].cross()
-    gdy[0].start()
-    gx[2].forward()
     a_qkv(1)
     a_heads(1)
     a_out(1)
+    gdy[0].finish()
+    gx[2].start()
+    gdy[1].start()
+    gdy[2].start()
+    ar1[1].cross()
+    ar1[0].back()
+    ar1[0].finish()
+    b_main(0)
+    gx[2].forward()
+    b_down(0)
+    b_up(0)
+    b_ffn(0)
+    b_prep(1)
+    units[0].relay(0)
+    gdy[1].forward()
+    gdy[1].finish()
+    b_sum(0)
+    rs1[0].cross()
     gx[2].finish()
-    ar1[0].back()
     a_norm(2)
-    gdy[0].forward()
-    ar1[1].cross()
-    gdy[1].start()
     a_qkv(2)
-    ar1[0].finish()
-    gdy[0].finish()
-    b_main(0)
-    b_ffn(0)
+    gdy[2].forward()
+    gdy[2].finish()
+    ar2[0].cross()
+    units[0].relay(1)
+    units[0].relay(2)
+    a_heads(2)
+    units[0].relay(3)
+    units[1].relay(0)
     ar1[1].back()
-    ar2[0].cross()
-    rs1[0].cross()
-    b_grad(0)
-    for copy in ffn_w[1]:
-        copy.start()
-    gdy[1].forward()
-    a_heads(2)
+    ar1[1].finish()
+    units[1].relay(1)
+    b_main(1)
+    b_down(1)
+    units[1].relay(2)
+    b_up(1)
+    b_ffn(1)
+    y_out(0)
+    b_sum(1)
+    units[0].finish()
     a_out(2)
+    units[1].relay(3)
+    units[2].relay(0)
+    rs1[1].cross()
+    ar1[2].cross()
     ar2[0].back()
-    grad_b.relay(0)
-    ar1[1].finish()
-    gdy[1].finish()
-    ar1[2].cross()
-    gdy[2].start()
-    b_main(1)
-    ar1[2].back()
-    b_ffn(1)
-    ar2[1].cross()
-    rs1[1].cross()
-    y_out(0)
-    b_grad(1)
-    for copy in ffn_w[2]:
-        copy.start()
-    gdy[2].forward()
+    ar2[0].finish()
+    units[2].relay(1)
     c_norm(0)
     c_heads(0)
+    c_sum(0)
+    units[2].relay(2)
+    units[2].relay(3)
+    c_prep(0)
+    c_grad(0)
+    units[3].relay(0)
+    units[1].finish()
+    ar2[1].cross()
+    y_out(1)
+    c_dn(0)
+    units[3].relay(1)
+    units[2].finish()
+    b_prep(2)
+    rs2[0].cross()
+    units[3].relay(2)
+    stats[0].cross()
+    ar1[2].back()
+    ar1[2].finish()
+    b_main(2)
+    units[3].relay(3)
+    units[4].relay(0)
+    units[4].relay(1)
+    b_down(2)
+    units[3].finish()
+    units[4].relay(2)
+    b_sum(2)
+    b_ffn(2)
+    units[4].relay(3)
+    last_norm(0)
     ar2[1].back()
-    c_norm_in(0)
-    rs2[0].cross()
-    stats[0].cross()
-    c_grad(0)
-    grad_b.finish(0)
-    grad_b.relay(1)
-    ar1[2].finish()
-    gdy[2].finish()
-    b_main(2)
-    b_ffn(2)
+    ar2[1].finish()
+    units[5].relay(0)
     ar2[2].cross()
+    b_up(2)
+    units[4].finish()
+    units[5].relay(1)
     rs1[2].cross()
-    grad_c.relay(0)
-    y_out(1)
-    b_grad(2)
-    last_norm(0)
     c_norm(1)
+    units[5].relay(2)
+    c_prep(1)
     c_heads(1)
+    c_grad(1)
+    units[5].relay(3)
+    units[6].relay(0)
     ar2[2].back()
-    c_norm_in(1)
+    ar2[2].finish()
+    c_sum(1)
+    c_dn(1)
     rs2[1].cross()
     stats[1].cross()
-    c_grad(1)
-    grad_b.finish(1)
-    grad_b.relay(2)
-    grad_c.finish(0)
+    units[6].relay(1)
+    units[6].relay(2)
+    units[5].finish()
     y_out(2)
+    units[6].relay(3)
     c_norm(2)
-    grad_c.relay(1)
+    units[7].relay(0)
+    last_norm(1)
+    small_send(0)
     c_heads(2)
-    c_norm_in(2)
+    small_relay(0)
+    units[7].relay(1)
+    c_grad(2)
+    c_prep(2)
+    units[6].finish()
+    units[7].relay(2)
+    units[7].relay(3)
+    c_sum(2)
+    c_dn(2)
     rs2[2].cross()
     stats[2].cross()
-    c_grad(2)
-    last_norm(1)
-    grad_b.finish(2)
-    grad_c.finish(1)
-    grad_c.relay(2)
+    units[8].relay(0)
+    units[8].relay(1)
+    units[7].finish()
+    units[8].relay(2)
     last_norm(2)
-    small_out()
-    grad_c.finish(2)
+    small_send(1)
+    units[8].relay(3)
+    small_relay(1)
+    small_finish(0)
+    units[8].finish()
+    small_finish(1)
     for copy in list(pending):
         sent(copy)
-    for grad in (grad_b, grad_c):
-        for copy in grad.hbm.get(TOWERS - 1, []):
+    for unit in units:
+        for copy in unit.hbm:
             copy.wait()
+
+
+def deliver(*refs):
+    count = 2 * TOWERS + 4
+    src, rows = refs[:count], refs[count]
+    dst = refs[count + 1 : 2 * count + 1]
+    qvb, outb, upb, downb, gains, shifts = refs[2 * count + 1 : 2 * count + 7]
+    room = refs[2 * count + 7 : 3 * count + 7]
+    in_sem, out_sem = refs[3 * count + 7 :]
+    reads = [pltpu.make_async_copy(src[i], room[i], in_sem.at[i]) for i in range(count)]
+    writes = [pltpu.make_async_copy(room[i], dst[i], out_sem.at[i]) for i in range(count)]
+    for copy in reads:
+        copy.start()
+    share = rows.shape[1]
+    for t in range(TOWERS):
+        for j in range(2):
+            qvb[t, j, :] = rows[small_row(t, j), :]
+            gains[t, j, :] = rows[small_row(t, 8 + j), :]
+            shifts[t, j, :] = rows[small_row(t, 10 + j), :]
+        outb[t, :] = rows[small_row(t, 2), :]
+        downb[t, :] = rows[small_row(t, 7), :]
+        for j in range(upb.shape[1] // share):
+            upb[t, j * share : (j + 1) * share] = rows[small_row(t, 3 + j), :]
+    for read, write in zip(reads, writes):
+        read.wait()
+        write.start()
+    for copy in writes:
+        copy.wait()
 
 
 def per_device(dp, tensor, *args):
@@ -836,19 +982,11 @@
     qkv_w, qv_b, out_w, out_b, up_w, up_b, down_w, down_b, gain, shift = args[5:15]
     plan = Plan(rows, (qkv_w, out_w, up_w), dp, tensor)
     width, share, hidden = plan.width, plan.share, plan.hidden
-    ratio = hidden // share
     nz = plan.nz
 
     turned = [jnp.transpose(x, (0, 2, 1)) for x in rows]
     turned_up = [jnp.transpose(x, (0, 2, 1)) for x in ups]
     wqkv = jnp.transpose(qkv_w, (0, 2, 3, 1)).reshape(TOWERS, 3 * share, width)
-    columns = jnp.concatenate(
-        [gain, shift, out_b[:, None], qv_b, down_b[:, None], up_b.reshape(TOWERS, ratio, share)],
-        axis=1,
-    ).reshape(TOWERS * COLS, share)
-    columns = jnp.pad(columns, ((0, 128 - TOWERS * COLS), (0, 0))).astype(F32)
-    lengths = jnp.concatenate([text_lengths, pair_lengths])
-
     vmem = pl.BlockSpec(memory_space=pltpu.VMEM)
     hbm = pl.BlockSpec(memory_space=pl.ANY)
     smem = pl.BlockSpec(memory_space=pltpu.SMEM)
@@ -856,8 +994,14 @@
     ins, specs = SimpleNamespace(), SimpleNamespace()
     ins.in_x, specs.in_x = turned, [hbm] * TOWERS
     ins.in_dy, specs.in_dy = turned_up, [hbm] * TOWERS
-    ins.prm, specs.prm = columns, vmem
-    ins.lengths, specs.lengths = lengths, smem
+    ins.in_text, specs.in_text = text_lengths, smem
+    ins.in_pair, specs.in_pair = pair_lengths, smem
+    ins.in_gain, specs.in_gain = gain, vmem
+    ins.in_shift, specs.in_shift = shift, vmem
+    ins.in_out_b, specs.in_out_b = out_b, vmem
+    ins.in_qv_b, specs.in_qv_b = qv_b, vmem
+    ins.in_down_b, specs.in_down_b = down_b, vmem
+    ins.in_up_b, specs.in_up_b = up_b, vmem
     ins.wqkv, specs.wqkv = wqkv, hbm
     ins.wout, specs.wout = out_w, hbm
     ins.wup, specs.wup = up_w, hbm
@@ -871,15 +1015,9 @@
         outs.o_out = Out(hbm, (TOWERS, share, plan.slab))
         outs.o_up = Out(hbm, (TOWERS, plan.slab, hidden))
         outs.o_down = Out(hbm, (TOWERS, plan.slab, hidden))
-        outs.o_qvb = Out(vmem, (TOWERS, 2, share))
-        outs.o_outb = Out(vmem, (TOWERS, share))
-        outs.o_upb = Out(vmem, (TOWERS * ratio, share))
-        outs.o_downb = Out(vmem, (TOWERS, share))
-        outs.o_gain = Out(vmem, (TOWERS, 2, share))
-        outs.o_bias = Out(vmem, (TOWERS, 2, share))
     else:
-        outs.o_g = [Out(hbm, (TOWERS, width, n), BF16) for n in plan.grad_lanes]
-        outs.o_small = Out(vmem, (share, 128))
+        outs.o_g = Out(hbm, (3, TOWERS, width, width), BF16)
+    outs.o_rows = Out(vmem, (SMALL, share))
 
     room = scratch(plan)
     in_refs, in_tree = flatten(vars(ins))
@@ -908,33 +1046,41 @@
     got = SimpleNamespace(**jax.tree.unflatten(out_tree, results))
 
     if not plan.fused:
-        sums_b, sums_c = [
-            lax.psum_scatter(g.astype(F32), "dp", scatter_dimension=1, tiled=True)
-            for g in got.o_g
-        ]
-        small = lax.psum(got.o_small, "dp").T[: TOWERS * COLS].reshape(TOWERS, COLS, share)
-        got.o_up, got.o_down = sums_b[:, :, :hidden], sums_b[:, :, hidden:]
-        slab = sums_c.shape[1]
-        qkv = sums_c[:, :, : 3 * share].reshape(TOWERS, slab, 3, share)
+        sums = lax.psum_scatter(got.o_g.astype(F32), "dp", scatter_dimension=2, tiled=True)
+        got.o_up, got.o_down = sums[UP], sums[DOWN]
+        qkv = sums[ATTN, :, :, : 3 * share].reshape(TOWERS, sums.shape[2], 3, share)
         got.o_qkv = jnp.transpose(qkv, (0, 2, 1, 3))
-        got.o_out = jnp.transpose(sums_c[:, :, 3 * share :], (0, 2, 1))
-        got.o_qvb, got.o_outb = small[:, 0:2], small[:, 2]
-        got.o_upb, got.o_downb = small[:, 3 : 3 + ratio], small[:, 7]
-        got.o_gain, got.o_bias = small[:, 8:10], small[:, 10:12]
-
+        got.o_out = jnp.transpose(sums[ATTN, :, :, 3 * share :], (0, 2, 1))
+        got.o_rows = lax.psum(got.o_rows, "dp")
+
+    big = [*got.o_y, *got.o_dx, got.o_qkv, got.o_out, got.o_up, got.o_down]
+    pairs = jax.ShapeDtypeStruct((TOWERS, 2, share), F32)
+    single = jax.ShapeDtypeStruct((TOWERS, share), F32)
+    small = [pairs, single, jax.ShapeDtypeStruct((TOWERS, hidden), F32), single, pairs, pairs]
+    count = len(big)
+    results = pl.pallas_call(
+        deliver,
+        out_shape=[jax.ShapeDtypeStruct(x.shape, x.dtype) for x in big] + small,
+        in_specs=[hbm] * count + [vmem],
+        out_specs=[hbm] * count + [vmem] * len(small),
+        scratch_shapes=[pltpu.VMEM(x.shape, x.dtype) for x in big]
+        + [pltpu.SemaphoreType.DMA((count,)), pltpu.SemaphoreType.DMA((count,))],
+        compiler_params=pltpu.CompilerParams(vmem_limit_bytes=67043328),
+    )(*big, got.o_rows)
+    rows, sums = results[: 2 * TOWERS], results[2 * TOWERS : count]
+    qvb, outb, upb, downb, gains, shifts = results[count:]
     return (
-        *[jnp.transpose(y, (0, 2, 1)) for y in got.o_y],
-        *[jnp.transpose(dx, (0, 2, 1)) for dx in got.o_dx],
-        jnp.transpose(got.o_qkv, (0, 2, 1, 3)),
-        got.o_qvb,
-        got.o_out,
-        got.o_outb,
-        got.o_up,
-        got.o_upb.reshape(TOWERS, hidden),
-        jnp.transpose(got.o_down, (0, 2, 1)),
-        got.o_downb,
-        got.o_gain,
-        got.o_bias,
+        *[jnp.transpose(x, (0, 2, 1)) for x in rows],
+        jnp.transpose(sums[0], (0, 2, 1, 3)),
+        qvb,
+        sums[1],
+        outb,
+        sums[2],
+        upb,
+        jnp.transpose(sums[3], (0, 2, 1)),
+        downb,
+        gains,
+        shifts,
     )
 
 

time: 250 us -> 186 us (0.74)
  Pallas kernels: 224 us -> 183 us
  local copies, waits for them, and re-layouts: 22 us -> 0 us
    pallas_call x1, Pallas kernels: 224 us -> 177 us  [per_device(): pl.pallas_call(body, out_shape=[jax.ShapeDtypeStruct(out.shape, out.dtype...]
    unnamed x31 -> x0, local copies, waits for them, and re-layouts: 17.5 us -> none
    pallas_call x0 -> x1, Pallas kernels: none -> 5.73 us  [per_device(): pl.pallas_call(deliver, out_shape=[jax.ShapeDtypeStruct(x.shape, x.dtype)...]
where the time goes in v2:
time: 186 us; the launch traced here: 185 us
  Pallas kernels  183 us (98%)
  between operations  2.13 us (1%)
    pallas_call x1, Pallas kernels, per_device(): pl.pallas_call(body, out_shape=[jax.ShapeDtypeStruct(out.shape, out.dtype...  177 us
    pallas_call x1, Pallas kernels, per_device(): pl.pallas_call(deliver, out_shape=[jax.ShapeDtypeStruct(x.shape, x.dtype)...  5.73 us

profile of v2, /device:TPU:0, one launch (start us, length us, event | category | flops | bytes accessed | tf_op | source)
XLA Modules:
  0.0 185.3 jit_solution(2978252031242944568)
XLA Ops:
  1.9 177.5 %layer.1 = (f32[3,96,768]{2,1,0:T(8,128)}, bf16[2,192,197]{2,1,0:T(8,128)(2,1)}, bf16[1,192,512]{2,1,0:T(8,128)(2,1)}, bf16[1,192,711]{2,1,0:T(8,128)(2,1)}, f32...) custom-call(bf16[3,192]{1,0:T(4,128)(2,1)} %refs_0_.1, ...), custom_call_target="tpu_custom_call" | custom-call | tf_op jit(solution)/shard_map/layer/pallas_call | solution.py:1035
  179.4 5.7 %shard_map.297 = (bf16[2,192,197]{2,1,0:T(8,128)(2,1)}, bf16[1,192,512]{2,1,0:T(8,128)(2,1)}, bf16[1,192,711]{2,1,0:T(8,128)(2,1)}, bf16[2,192,197]{2,1,0:T(8,12...) custom-call(bf16[2,192,197]{2,1,0:T(8,128)(2,1)} %get-tuple-element., ...), custom_call_target="tpu_custom_call" | custom-call | tf_op jit(solution)/shard_map/pallas_call | solution.py:1061

commit v3 on v2

--- a/solution.py
+++ b/solution.py
@@ -19,12 +19,13 @@
     (0, UP),
     (1, DOWN),
     (1, UP),
-    (0, ATTN),
     (2, DOWN),
     (2, UP),
+    (0, ATTN),
     (1, ATTN),
     (2, ATTN),
 )
+Z_FIRST = (1,)
 TILE = 256
 COLS = 12
 N_REMOTE = 160
@@ -65,7 +66,7 @@
         self.pad = (3 * self.share) % TILE
         assert tensor == 4 and self.width == 4 * self.share
         assert self.pad + self.share == TILE and self.hidden == self.width
-        self.fused = dp % 2 == 0 and dp > 1 and self.width % (16 * dp) == 0
+        self.fused = dp == 8 and self.width % (16 * dp) == 0
         self.nz = dp // 2 if self.fused else 1
         self.slab = self.width // dp if self.fused else self.width
         self.halves = 2 if self.fused else 1
@@ -116,13 +117,14 @@
     if plan.fused:
         k.g_y = vm(RING, nz, plan.slab, width)
         k.g_z = vm(RING, nz, plan.slab, width)
-        k.g_far = vm(len(UNITS), max(nz - 1, 1), plan.slab, width)
+        k.g_far = vm(len(UNITS), 3, plan.slab, width)
+        k.zf_near = vm(2, 2, plan.slab, width)
+        k.zf_far, k.zf_y = vm(2, plan.slab, width), vm(plan.slab, width)
         k.s_ffn = vm(2, plan.slab, hidden, dtype=F32)
         k.s_qkv = vm(3, plan.slab, share, dtype=F32)
         k.s_out = vm(share, plan.slab, dtype=F32)
-        k.rows = [vm(n, share, dtype=F32) for n in (EARLY, LATE)]
-        k.rows_y = [vm(n, share, dtype=F32) for n in (EARLY, LATE)]
-        k.rows_z = [vm(nz, n, share, dtype=F32) for n in (EARLY, LATE)]
+        k.rows = [vm(3, n, share, dtype=F32) for n in (EARLY, LATE)]
+        k.rows_in = [vm(3, n, share, dtype=F32) for n in (EARLY, LATE)]
     k.wqkv_v, k.wout_v = vm(2, 3 * share, width), vm(2, share, width)
     k.wup_v, k.wdown_v = vm(width, hidden), vm(hidden, width)
     k.up_t, k.down_t = vm(hidden, width), vm(width, hidden)
@@ -130,6 +132,9 @@
     k.work_h, k.work_m = vm(width, most), vm(share, most)
     k.pown, k.pfull = vm(share, 128, dtype=F32), vm(width, 128)
     k.prm, k.small = vm(128, share, dtype=F32), vm(share, 128, dtype=F32)
+    k.v_y = [vm(e, share, n) for e, n in zip(plan.examples, plan.length)]
+    k.v_dx = [vm(e, share, n) for e, n in zip(plan.examples, plan.length)]
+    k.row_sem = dma((2 * TOWERS,))
     k.in_sem, k.w_sem, k.part_sem = dma((2 * TOWERS,)), dma((18,)), dma(())
     k.send_sem, k.recv_sem = dma((N_REMOTE,)), dma((N_REMOTE,))
     return k
@@ -150,12 +155,11 @@
     across = (dp_at, lax.rem(me + 2, 4))
     y_peer = (dp_at + 1 - 2 * y_at, me)
 
-    def z_index(k):
-        return lax.rem(z_at + k, nz)
-
-    def z_peer(k):
-        return (z_index(k) * 2 + y_at, me)
-
+    z_near = z_at + 1 - 2 * lax.rem(z_at, 2)
+    z_far, z_near_far = lax.rem(z_at + 2, 4), lax.rem(z_near + 2, 4)
+    near_dev, far_dev = (z_near * 2 + y_at, me), (z_far * 2 + y_at, me)
+
+    row_copies = []
     counter = [0]
     pending = []
 
@@ -311,7 +315,12 @@
             self.at, self.t, self.kind = at, t, kind
             self.slot = at % RING
             self.all = r.g_all.at[self.slot]
-            self.y_copies, self.z_copies, self.hbm = [], [], []
+            self.sums = r.g_z.at[self.slot] if plan.fused else None
+            self.first, self.z_copies, self.hbm = [], [], []
+            self.z_first = at in Z_FIRST
+
+        def across_z(self, src, dst, device):
+            self.z_copies.append(launch(remote(src, dst, device)))
 
         def send(self):
             if not plan.fused:
@@ -322,42 +331,79 @@
                 return
             if self.at >= RING:
                 pl.semaphore_wait(r.credit.at[self.slot], 1)
-            for j in range(nz):
-                at = z_index(1 + j)
-                src, dst = self.all.at[1 - y_at, at], r.g_y.at[self.slot, at]
-                self.y_copies.append(launch(remote(src, dst, y_peer)))
-
-        def relay(self, quarter):
-            if plan.fused:
-                for j in range(nz * quarter // 4, nz * (quarter + 1) // 4):
-                    self.relay_piece(j)
-
-        def relay_piece(self, j):
-            if j == 0 and self.at >= RING:
+            if self.z_first:
+                for i, blk in enumerate((z_near_far, z_near)):
+                    for yy in range(2):
+                        dst = r.zf_near.at[i, yy]
+                        self.first.append(launch(remote(self.all.at[yy, blk], dst, near_dev)))
+                return
+            for blk in (z_near_far, z_near, z_far, z_at):
+                src, dst = self.all.at[1 - y_at, blk], r.g_y.at[self.slot, blk]
+                self.first.append(launch(remote(src, dst, y_peer)))
+
+        def relay(self, step):
+            if not plan.fused:
+                return
+            if step == 0 and self.at >= RING:
                 for copy in units[self.at - RING].z_copies:
                     sent(copy)
-            at = z_index(1 + j)
-            sums = r.g_z.at[self.slot, at]
-            self.y_copies[j].wait_recv()
-            total = self.all[y_at, at].astype(F32) + r.g_y[self.slot, at].astype(F32)
-            sums[...] = total.astype(BF16)
-            if j < nz - 1:
-                dst = r.g_far.at[self.at, j]
-                self.z_copies.append(launch(remote(sums, dst, z_peer(1 + j))))
-                return
-            for copy in self.y_copies:
-                sent(copy)
-            if self.at + RING < len(units):
-                credit = r.credit.at[self.slot]
-                pl.semaphore_signal(credit, inc=1, device_id=y_peer, device_id_type=MESH)
+            if self.z_first:
+                self.relay_z(step)
+            else:
+                self.relay_y(step)
+            if step == 3:
+                for copy in self.first:
+                    sent(copy)
+                if self.at + RING < len(units):
+                    credit = r.credit.at[self.slot]
+                    pl.semaphore_signal(credit, inc=1, device_id=y_peer, device_id_type=MESH)
+
+        def relay_y(self, step):
+            blk = (z_near_far, z_near, z_far, z_at)[step]
+            self.first[step].wait_recv()
+            total = self.all[y_at, blk].astype(F32) + r.g_y[self.slot, blk].astype(F32)
+            land = r.g_far.at[self.at]
+            if step == 2:
+                self.z_copies[0].wait_recv()
+                total = total + r.g_far[self.at, 1].astype(F32)
+            self.sums[blk] = total.astype(BF16)
+            if step == 0:
+                self.across_z(self.sums.at[blk], land.at[1], near_dev)
+            if step == 1:
+                self.across_z(self.sums.at[blk], land.at[0], near_dev)
+            if step == 2:
+                self.across_z(self.sums.at[blk], land.at[2], far_dev)
+
+        def relay_z(self, step):
+            def known(i, yy, blk):
+                return self.all[yy, blk].astype(F32) + r.zf_near[i, yy].astype(F32)
+
+            if step == 0:
+                for yy in range(2):
+                    self.first[yy].wait_recv()
+                    self.sums[yy] = known(0, yy, z_far).astype(BF16)
+                    self.across_z(self.sums.at[yy], r.zf_far.at[yy], far_dev)
+            if step == 1:
+                for yy in range(2):
+                    self.first[2 + yy].wait_recv()
+                    self.z_copies[yy].wait_recv()
+                for at, yy in ((2, 1 - y_at), (3, y_at)):
+                    total = known(1, yy, z_at) + r.zf_far[yy].astype(F32)
+                    self.sums[at] = total.astype(BF16)
+                self.across_z(self.sums.at[2], r.zf_y, y_peer)
 
         def finish(self):
             if not plan.fused:
                 return
-            total = r.g_z[self.slot, z_at].astype(F32)
-            for j in range(nz - 1):
-                self.z_copies[j].wait_recv()
-                total = total + r.g_far[self.at, j].astype(F32)
+            if self.z_first:
+                self.z_copies[2].wait_recv()
+                total = self.sums[3].astype(F32) + r.zf_y[...].astype(F32)
+            else:
+                self.z_copies[1].wait_recv()
+                self.z_copies[2].wait_recv()
+                total = self.sums[z_at].astype(F32)
+                for i in (0, 2):
+                    total = total + r.g_far[self.at, i].astype(F32)
             t, sem = self.t, r.out_sem
             for before in units[: self.at]:
                 if before.kind == self.kind:
@@ -599,7 +645,9 @@
         padded = plan.padded[t]
         for e in range(plan.examples[t]):
             out = value[:, e * padded : e * padded + plan.length[t]]
-            r.o_y[t][e] = out.astype(BF16)
+            r.v_y[t][e] = out.astype(BF16)
+        row_copies.append(pltpu.make_async_copy(r.v_y[t], r.o_y[t], r.row_sem.at[t]))
+        row_copies[-1].start()
 
     def c_norm(t):
         for copy in attn_w[TOWERS + t]:
@@ -726,7 +774,9 @@
         padded = plan.padded[t]
         for e in range(plan.examples[t]):
             out = value[:, e * padded : e * padded + plan.length[t]]
-            r.o_dx[t][e] = out.astype(BF16)
+            r.v_dx[t][e] = out.astype(BF16)
+        row_copies.append(pltpu.make_async_copy(r.v_dx[t], r.o_dx[t], r.row_sem.at[TOWERS + t]))
+        row_copies[-1].start()
         keep_sum(t, 8, dn * xhat)
         keep_sum(t, 10, dn)
 
@@ -737,64 +787,64 @@
         if not plan.fused:
             r.o_rows[first:last] = part
             return
-        r.rows[late][...] = part
-        small_y[late] = launch(remote(r.rows[late], r.rows_y[late], y_peer))
-
-    def small_relay(late):
+        r.rows[late][0] = part
+        small_step(late, 0)
+
+    def small_step(late, step):
+        rows, land = r.rows[late].at[step], r.rows_in[late].at[step]
+        device = (y_peer, near_dev, far_dev)[step]
+        small_copies[late].append(launch(remote(rows, land, device)))
+
+    def small_relay(late, step):
         if not plan.fused:
             return
-        small_y[late].wait_recv()
-        r.rows_z[late][z_at] = r.rows[late][...] + r.rows_y[late][...]
-        for k in range(1, nz):
-            slot = r.rows_z[late].at[z_at]
-            small_z[late].append(launch(remote(slot, slot, z_peer(k))))
+        small_copies[late][step - 1].wait_recv()
+        r.rows[late][step] = r.rows[late][step - 1] + r.rows_in[late][step - 1]
+        small_step(late, step)
 
     def small_finish(late):
         if not plan.fused:
             return
-        for copy in small_z[late]:
-            copy.wait_recv()
-        total = r.rows_z[late][0]
-        for k in range(1, nz):
-            total = total + r.rows_z[late][k]
+        small_copies[late][2].wait_recv()
+        total = r.rows[late][2] + r.rows_in[late][2]
         if late:
             r.o_rows[EARLY : EARLY + LATE] = total
         else:
             r.o_rows[:EARLY] = total
 
-    small_y, small_z = [None, None], [[], []]
+    small_copies = [[], []]
 
     barrier = pltpu.get_barrier_semaphore()
     partners = [sibling, across]
     if plan.fused:
-        partners += [y_peer] + [z_peer(k) for k in range(1, nz)]
+        partners += [y_peer, near_dev, far_dev]
     for device in partners:
         pl.semaphore_signal(barrier, inc=1, device_id=device, device_id_type=MESH)
     loads = [
         pltpu.make_async_copy(src[t], dst[t], r.in_sem.at[i * TOWERS + t])
-        for i, (src, dst) in enumerate(((r.in_x, r.o_y), (r.in_dy, r.o_dx)))
+        for i, (src, dst) in enumerate(((r.in_x, r.v_y), (r.in_dy, r.v_dx)))
         for t in range(TOWERS)
     ]
     for copy in loads + attn_w[0] + ffn_w[0] + attn_w[1]:
         copy.start()
     param_rows()
     loads[0].wait()
-    stage_in(r.x[0], 0, r.o_y[0])
+    stage_in(r.x[0], 0, r.v_y[0])
     pl.semaphore_wait(barrier, len(partners))
     gp.start()
     gx[0].start()
     for t in range(1, TOWERS):
         loads[t].wait()
-        stage_in(r.x[t], t, r.o_y[t])
+        stage_in(r.x[t], t, r.v_y[t])
     for t in range(TOWERS):
         loads[TOWERS + t].wait()
-        stage_in(r.dy[t], t, r.o_dx[t])
+        stage_in(r.dy[t], t, r.v_dx[t])
     r.small[...] = jnp.zeros_like(r.small)
+    gx[1].start()
     gp.forward()
-    gx[1].start()
     gp.finish()
+    b_prep(0)
     gdy[0].start()
-    b_prep(0)
     gx[0].forward()
     gx[0].finish()
     a_norm(0)
@@ -802,150 +852,154 @@
     a_heads(0)
     a_out(0)
     ar1[0].cross()
+    gx[2].start()
+    gx[1].forward()
     gdy[0].forward()
-    gx[1].forward()
     gx[1].finish()
+    gdy[0].finish()
     a_norm(1)
     a_qkv(1)
     a_heads(1)
     a_out(1)
-    gdy[0].finish()
-    gx[2].start()
+    ar1[1].cross()
     gdy[1].start()
     gdy[2].start()
-    ar1[1].cross()
     ar1[0].back()
     ar1[0].finish()
     b_main(0)
-    gx[2].forward()
     b_down(0)
     b_up(0)
+    gx[2].forward()
     b_ffn(0)
     b_prep(1)
-    units[0].relay(0)
-    gdy[1].forward()
-    gdy[1].finish()
-    b_sum(0)
-    rs1[0].cross()
     gx[2].finish()
     a_norm(2)
     a_qkv(2)
-    gdy[2].forward()
-    gdy[2].finish()
-    ar2[0].cross()
+    b_sum(0)
+    a_heads(2)
+    gdy[1].forward()
+    ar1[1].back()
+    a_out(2)
+    units[0].relay(0)
+    gdy[1].finish()
+    ar1[1].finish()
+    b_main(1)
+    b_down(1)
+    b_sum(1)
+    ar1[2].cross()
     units[0].relay(1)
     units[0].relay(2)
-    a_heads(2)
     units[0].relay(3)
+    gdy[2].forward()
+    rs1[0].cross()
     units[1].relay(0)
-    ar1[1].back()
-    ar1[1].finish()
+    gdy[2].finish()
+    b_up(1)
+    units[0].finish()
+    b_ffn(1)
+    b_prep(2)
+    ar2[0].cross()
+    ar1[2].back()
+    ar1[2].finish()
     units[1].relay(1)
-    b_main(1)
-    b_down(1)
     units[1].relay(2)
-    b_up(1)
-    b_ffn(1)
-    y_out(0)
-    b_sum(1)
-    units[0].finish()
-    a_out(2)
     units[1].relay(3)
     units[2].relay(0)
+    ar2[1].cross()
+    units[2].relay(1)
+    b_main(2)
+    b_sum(2)
+    units[2].relay(2)
     rs1[1].cross()
-    ar1[2].cross()
+    b_down(2)
+    units[2].relay(3)
+    units[3].relay(0)
+    b_ffn(2)
+    b_up(2)
+    units[3].relay(1)
+    units[1].finish()
     ar2[0].back()
+    rs1[2].cross()
     ar2[0].finish()
-    units[2].relay(1)
+    y_out(0)
     c_norm(0)
+    ar2[1].back()
+    units[3].relay(2)
+    units[3].relay(3)
     c_heads(0)
     c_sum(0)
-    units[2].relay(2)
-    units[2].relay(3)
+    units[2].finish()
     c_prep(0)
-    c_grad(0)
-    units[3].relay(0)
-    units[1].finish()
-    ar2[1].cross()
-    y_out(1)
-    c_dn(0)
-    units[3].relay(1)
-    units[2].finish()
-    b_prep(2)
-    rs2[0].cross()
-    units[3].relay(2)
-    stats[0].cross()
-    ar1[2].back()
-    ar1[2].finish()
-    b_main(2)
-    units[3].relay(3)
+    ar2[2].cross()
     units[4].relay(0)
     units[4].relay(1)
-    b_down(2)
+    c_grad(0)
+    c_dn(0)
+    units[4].relay(2)
+    units[4].relay(3)
     units[3].finish()
-    units[4].relay(2)
-    b_sum(2)
-    b_ffn(2)
-    units[4].relay(3)
-    last_norm(0)
-    ar2[1].back()
+    units[5].relay(0)
+    units[5].relay(1)
+    rs2[0].cross()
+    y_out(1)
+    y_out(2)
     ar2[1].finish()
-    units[5].relay(0)
-    ar2[2].cross()
-    b_up(2)
-    units[4].finish()
-    units[5].relay(1)
-    rs1[2].cross()
     c_norm(1)
-    units[5].relay(2)
     c_prep(1)
     c_heads(1)
-    c_grad(1)
-    units[5].relay(3)
-    units[6].relay(0)
-    ar2[2].back()
-    ar2[2].finish()
     c_sum(1)
     c_dn(1)
+    c_grad(1)
+    stats[0].cross()
+    ar2[2].back()
+    units[5].relay(2)
+    units[5].relay(3)
+    ar2[2].finish()
+    c_norm(2)
+    units[6].relay(0)
+    units[6].relay(1)
     rs2[1].cross()
     stats[1].cross()
-    units[6].relay(1)
+    c_heads(2)
+    units[4].finish()
     units[6].relay(2)
+    c_prep(2)
+    c_dn(2)
+    units[6].relay(3)
+    units[7].relay(0)
+    units[7].relay(1)
+    rs2[2].cross()
+    last_norm(1)
+    last_norm(0)
+    small_send(0)
+    c_grad(2)
     units[5].finish()
-    y_out(2)
-    units[6].relay(3)
-    c_norm(2)
-    units[7].relay(0)
-    last_norm(1)
-    small_send(0)
-    c_heads(2)
-    small_relay(0)
-    units[7].relay(1)
-    c_grad(2)
-    c_prep(2)
-    units[6].finish()
+    small_relay(0, 1)
+    stats[2].cross()
     units[7].relay(2)
     units[7].relay(3)
+    last_norm(2)
+    units[6].finish()
     c_sum(2)
-    c_dn(2)
-    rs2[2].cross()
-    stats[2].cross()
+    small_relay(0, 2)
     units[8].relay(0)
     units[8].relay(1)
+    small_send(1)
+    small_relay(1, 1)
+    units[8].relay(2)
     units[7].finish()
-    units[8].relay(2)
-    last_norm(2)
-    small_send(1)
+    small_relay(1, 2)
     units[8].relay(3)
-    small_relay(1)
+    units[8].finish()
     small_finish(0)
-    units[8].finish()
     small_finish(1)
     for copy in list(pending):
         sent(copy)
     for unit in units:
         for copy in unit.hbm:
             copy.wait()
+    for copy in row_copies:
+        copy.wait()
 
 
 def deliver(*refs):
@@ -1008,8 +1062,8 @@
     ins.wdown, specs.wdown = down_w, hbm
 
     outs = SimpleNamespace()
-    outs.o_y = [Out(vmem, x.shape, BF16) for x in turned]
-    outs.o_dx = [Out(vmem, x.shape, BF16) for x in turned]
+    outs.o_y = [Out(hbm, x.shape, BF16) for x in turned]
+    outs.o_dx = [Out(hbm, x.shape, BF16) for x in turned]
     if plan.fused:
         outs.o_qkv = Out(hbm, (TOWERS, 3, plan.slab, share))
         outs.o_out = Out(hbm, (TOWERS, share, plan.slab))

time: 186 us -> 176 us (0.946)
  Pallas kernels: 183 us -> 174 us
    pallas_call x1, Pallas kernels: 177 us -> 168 us  [per_device(): pl.pallas_call(body, out_shape=[jax.ShapeDtypeStruct(out.shape, out.dtype...]
where the time goes in v3:
time: 176 us
  Pallas kernels  174 us (99%)
  between operations  2.13 us (1%)
    pallas_call x1, Pallas kernels, per_device(): pl.pallas_call(body, out_shape=[jax.ShapeDtypeStruct(out.shape, out.dtype...  168 us
    pallas_call x1, Pallas kernels, per_device(): pl.pallas_call(deliver, out_shape=[jax.ShapeDtypeStruct(x.shape, x.dtype)...  5.73 us

profile of v3, /device:TPU:0, one launch (start us, length us, event | category | flops | bytes accessed | tf_op | source)
XLA Modules:
  0.0 176.0 jit_solution(16158792148790788919)
XLA Ops:
  1.9 168.2 %layer.1 = (f32[3,96,768]{2,1,0:T(8,128)}, bf16[2,192,197]{2,1,0:T(8,128)(2,1)}, bf16[1,192,512]{2,1,0:T(8,128)(2,1)}, bf16[1,192,711]{2,1,0:T(8,128)(2,1)}, f32...) custom-call(bf16[3,192]{1,0:T(4,128)(2,1)} %refs_0_.1, ...), custom_call_target="tpu_custom_call" | custom-call | tf_op jit(solution)/shard_map/layer/pallas_call | solution.py:1089
  170.1 5.7 %shard_map.297 = (bf16[2,192,197]{2,1,0:T(8,128)(2,1)}, bf16[1,192,512]{2,1,0:T(8,128)(2,1)}, bf16[1,192,711]{2,1,0:T(8,128)(2,1)}, bf16[2,192,197]{2,1,0:T(8,12...) custom-call(bf16[2,192,197]{2,1,0:T(8,128)(2,1)} %get-tuple-element., ...), custom_call_target="tpu_custom_call" | custom-call | tf_op jit(solution)/shard_map/pallas_call | solution.py:1115

commit v4 on v3

--- a/solution.py
+++ b/solution.py
@@ -25,10 +25,10 @@
     (1, ATTN),
     (2, ATTN),
 )
-Z_FIRST = (1,)
+Z_FIRST = (2,)
 TILE = 256
 COLS = 12
-N_REMOTE = 160
+N_REMOTE = 132
 EARLY, LATE = 32, 8
 SMALL = EARLY + LATE
 LATE_COLS = (0, 1, 2, 8, 9, 10, 11)
@@ -840,158 +840,158 @@
         loads[TOWERS + t].wait()
         stage_in(r.dy[t], t, r.v_dx[t])
     r.small[...] = jnp.zeros_like(r.small)
-    gx[1].start()
     gp.forward()
     gp.finish()
-    b_prep(0)
     gdy[0].start()
     gx[0].forward()
+    gx[1].start()
     gx[0].finish()
     a_norm(0)
     a_qkv(0)
     a_heads(0)
     a_out(0)
+    gdy[0].forward()
     ar1[0].cross()
-    gx[2].start()
     gx[1].forward()
-    gdy[0].forward()
     gx[1].finish()
     gdy[0].finish()
     a_norm(1)
     a_qkv(1)
     a_heads(1)
+    gx[2].start()
     a_out(1)
+    b_prep(0)
     ar1[1].cross()
-    gdy[1].start()
-    gdy[2].start()
     ar1[0].back()
     ar1[0].finish()
     b_main(0)
     b_down(0)
-    b_up(0)
+    b_ffn(0)
+    b_sum(0)
     gx[2].forward()
-    b_ffn(0)
     b_prep(1)
+    gdy[1].start()
+    gdy[2].start()
     gx[2].finish()
     a_norm(2)
     a_qkv(2)
-    b_sum(0)
+    b_up(0)
+    units[0].relay(0)
+    units[0].relay(1)
     a_heads(2)
-    gdy[1].forward()
-    ar1[1].back()
-    a_out(2)
-    units[0].relay(0)
-    gdy[1].finish()
-    ar1[1].finish()
-    b_main(1)
-    b_down(1)
-    b_sum(1)
-    ar1[2].cross()
-    units[0].relay(1)
     units[0].relay(2)
     units[0].relay(3)
+    a_out(2)
+    ar1[2].cross()
+    units[1].relay(0)
+    ar1[1].back()
+    ar1[1].finish()
+    gdy[1].forward()
+    gdy[1].finish()
+    units[1].relay(1)
+    b_main(1)
+    units[1].relay(2)
+    ar2[0].cross()
+    b_down(1)
+    b_up(1)
+    b_ffn(1)
+    units[1].relay(3)
+    b_sum(1)
+    b_prep(2)
     gdy[2].forward()
     rs1[0].cross()
-    units[1].relay(0)
+    ar1[2].back()
+    units[0].finish()
     gdy[2].finish()
-    b_up(1)
-    units[0].finish()
-    b_ffn(1)
-    b_prep(2)
-    ar2[0].cross()
-    ar1[2].back()
     ar1[2].finish()
-    units[1].relay(1)
-    units[1].relay(2)
-    units[1].relay(3)
+    b_main(2)
+    b_down(2)
+    rs1[1].cross()
     units[2].relay(0)
+    b_sum(2)
     ar2[1].cross()
-    units[2].relay(1)
-    b_main(2)
-    b_sum(2)
-    units[2].relay(2)
-    rs1[1].cross()
-    b_down(2)
-    units[2].relay(3)
-    units[3].relay(0)
-    b_ffn(2)
-    b_up(2)
-    units[3].relay(1)
     units[1].finish()
     ar2[0].back()
-    rs1[2].cross()
+    units[3].relay(0)
+    y_out(1)
+    ar2[2].cross()
+    units[3].relay(1)
+    b_ffn(2)
+    y_out(0)
+    units[2].relay(1)
+    units[2].relay(2)
+    units[4].relay(0)
+    units[2].relay(3)
+    b_up(2)
     ar2[0].finish()
-    y_out(0)
+    units[3].relay(2)
     c_norm(0)
-    ar2[1].back()
-    units[3].relay(2)
-    units[3].relay(3)
+    c_prep(0)
+    units[4].relay(1)
     c_heads(0)
     c_sum(0)
+    c_dn(0)
+    ar2[1].back()
+    units[4].relay(2)
     units[2].finish()
-    c_prep(0)
-    ar2[2].cross()
-    units[4].relay(0)
-    units[4].relay(1)
+    units[3].relay(3)
+    units[5].relay(0)
+    ar2[1].finish()
+    rs1[2].cross()
     c_grad(0)
-    c_dn(0)
-    units[4].relay(2)
-    units[4].relay(3)
-    units[3].finish()
-    units[5].relay(0)
-    units[5].relay(1)
-    rs2[0].cross()
-    y_out(1)
-    y_out(2)
-    ar2[1].finish()
     c_norm(1)
     c_prep(1)
     c_heads(1)
+    c_dn(1)
+    units[4].relay(3)
+    rs2[0].cross()
+    units[3].finish()
     c_sum(1)
-    c_dn(1)
+    ar2[2].back()
+    units[5].relay(1)
     c_grad(1)
+    units[6].relay(0)
+    y_out(2)
+    rs2[1].cross()
     stats[0].cross()
-    ar2[2].back()
-    units[5].relay(2)
-    units[5].relay(3)
     ar2[2].finish()
     c_norm(2)
-    units[6].relay(0)
+    units[4].finish()
     units[6].relay(1)
-    rs2[1].cross()
+    units[5].relay(2)
+    c_heads(2)
+    last_norm(0)
+    c_prep(2)
+    units[7].relay(0)
     stats[1].cross()
-    c_heads(2)
-    units[4].finish()
+    c_dn(2)
+    rs2[2].cross()
     units[6].relay(2)
-    c_prep(2)
-    c_dn(2)
-    units[6].relay(3)
-    units[7].relay(0)
-    units[7].relay(1)
-    rs2[2].cross()
+    c_sum(2)
+    units[5].relay(3)
     last_norm(1)
-    last_norm(0)
     small_send(0)
     c_grad(2)
+    units[7].relay(1)
+    units[7].relay(2)
+    stats[2].cross()
+    last_norm(2)
+    units[6].relay(3)
+    small_send(1)
+    units[6].finish()
     units[5].finish()
     small_relay(0, 1)
-    stats[2].cross()
-    units[7].relay(2)
-    units[7].relay(3)
-    last_norm(2)
-    units[6].finish()
-    c_sum(2)
+    units[8].relay(0)
     small_relay(0, 2)
-    units[8].relay(0)
     units[8].relay(1)
-    small_send(1)
     small_relay(1, 1)
     units[8].relay(2)
+    units[8].relay(3)
+    units[7].relay(3)
     units[7].finish()
     small_relay(1, 2)
-    units[8].relay(3)
+    small_finish(0)
     units[8].finish()
-    small_finish(0)
     small_finish(1)
     for copy in list(pending):
         sent(copy)

time: 176 us -> 171 us (0.972)
  Pallas kernels: 174 us -> 169 us
    pallas_call x1, Pallas kernels: 168 us -> 163 us  [per_device(): pl.pallas_call(body, out_shape=[jax.ShapeDtypeStruct(out.shape, out.dtype...]
where the time goes in v4:
time: 171 us
  Pallas kernels  169 us (99%)
  between operations  2.13 us (1%)
    pallas_call x1, Pallas kernels, per_device(): pl.pallas_call(body, out_shape=[jax.ShapeDtypeStruct(out.shape, out.dtype...  163 us
    pallas_call x1, Pallas kernels, per_device(): pl.pallas_call(deliver, out_shape=[jax.ShapeDtypeStruct(x.shape, x.dtype)...  5.73 us

profile of v4, /device:TPU:0, one launch (start us, length us, event | category | flops | bytes accessed | tf_op | source)
XLA Modules:
  0.0 171.2 jit_solution(2919900866575535501)
XLA Ops:
  1.9 163.4 %layer.1 = (f32[3,96,768]{2,1,0:T(8,128)}, bf16[2,192,197]{2,1,0:T(8,128)(2,1)}, bf16[1,192,512]{2,1,0:T(8,128)(2,1)}, bf16[1,192,711]{2,1,0:T(8,128)(2,1)}, f32...) custom-call(bf16[3,192]{1,0:T(4,128)(2,1)} %refs_0_.1, ...), custom_call_target="tpu_custom_call" | custom-call | tf_op jit(solution)/shard_map/layer/pallas_call | solution.py:1089
  165.3 5.7 %shard_map.297 = (bf16[2,192,197]{2,1,0:T(8,128)(2,1)}, bf16[1,192,512]{2,1,0:T(8,128)(2,1)}, bf16[1,192,711]{2,1,0:T(8,128)(2,1)}, bf16[2,192,197]{2,1,0:T(8,12...) custom-call(bf16[2,192,197]{2,1,0:T(8,128)(2,1)} %get-tuple-element., ...), custom_call_target="tpu_custom_call" | custom-call | tf_op jit(solution)/shard_map/pallas_call | solution.py:1115

commit v5 on v4

--- a/solution.py
+++ b/solution.py
@@ -913,7 +913,6 @@
     units[1].finish()
     ar2[0].back()
     units[3].relay(0)
-    y_out(1)
     ar2[2].cross()
     units[3].relay(1)
     b_ffn(2)
@@ -939,6 +938,7 @@
     ar2[1].finish()
     rs1[2].cross()
     c_grad(0)
+    y_out(1)
     c_norm(1)
     c_prep(1)
     c_heads(1)
@@ -975,8 +975,8 @@
     units[7].relay(1)
     units[7].relay(2)
     stats[2].cross()
+    units[6].relay(3)
     last_norm(2)
-    units[6].relay(3)
     small_send(1)
     units[6].finish()
     units[5].finish()

time: 171 us -> 171 us (level)
  no operation moved by 1% of the time
where the time goes in v5:
time: 171 us; the launch traced here: 170 us
  Pallas kernels  168 us (98%)
  between operations  2.13 us (1%)
    pallas_call x1, Pallas kernels, per_device(): pl.pallas_call(body, out_shape=[jax.ShapeDtypeStruct(out.shape, out.dtype...  163 us
    pallas_call x1, Pallas kernels, per_device(): pl.pallas_call(deliver, out_shape=[jax.ShapeDtypeStruct(x.shape, x.dtype)...  5.73 us

profile of v5, /device:TPU:0, one launch (start us, length us, event | category | flops | bytes accessed | tf_op | source)
XLA Modules:
  0.0 170.4 jit_solution(9119307964431178380)
XLA Ops:
  1.9 162.6 %layer.1 = (f32[3,96,768]{2,1,0:T(8,128)}, bf16[2,192,197]{2,1,0:T(8,128)(2,1)}, bf16[1,192,512]{2,1,0:T(8,128)(2,1)}, bf16[1,192,711]{2,1,0:T(8,128)(2,1)}, f32...) custom-call(bf16[3,192]{1,0:T(4,128)(2,1)} %refs_0_.1, ...), custom_call_target="tpu_custom_call" | custom-call | tf_op jit(solution)/shard_map/layer/pallas_call | solution.py:1089
  164.5 5.7 %shard_map.297 = (bf16[2,192,197]{2,1,0:T(8,128)(2,1)}, bf16[1,192,512]{2,1,0:T(8,128)(2,1)}, bf16[1,192,711]{2,1,0:T(8,128)(2,1)}, bf16[2,192,197]{2,1,0:T(8,12...) custom-call(bf16[2,192,197]{2,1,0:T(8,128)(2,1)} %get-tuple-element., ...), custom_call_target="tpu_custom_call" | custom-call | tf_op jit(solution)/shard_map/pallas_call | solution.py:1115
